TPU v7x, 512 devices: a whole 4x8x8 slice. The times are simulated.
512 devices in a mesh: seq: 64 (over x, z, core), head: 8 (over y).
Axes of the slice: x: 4, y: 8, z: 8, core: 2. Of those that a mesh axis runs over, the one named last changes fastest.
Arguments:
- queries: bfloat16 [65536, 128], P('seq'), may hold values from -0.59765625 to 0.59765625
- key_rows: bfloat16 [65536, 128], P('seq'), may hold values from -0.59765625 to 0.59765625
- value_rows: bfloat16 [65536, 4096], P('seq', 'head'), may hold values from -0.119628906 to 0.119628906
- out_grad: bfloat16 [65536, 4096], P('seq', 'head'), may hold values from -0.29882812 to 0.29882812
- level_index: int32 [65536, 7], P('seq'), may hold values from 0 to 7
- level_table: float32 [7, 8, 64], P(None, None, 'head'), may hold values from 0.25 to 2.5
Outputs:
- query_grad: bfloat16 [65536, 128], P('seq')
- key_grad: bfloat16 [65536, 128], P('seq')
- value_grad: bfloat16 [65536, 4096], P('seq', 'head')
All inputs are finite; a program needn't handle non-finite values.
Results may differ from a plain program's by a relative error of at most 0.018.
Values may be sent and summed in bfloat16 or wider, within the bound.
A program may use at most 128 MiB of HBM per device.

v0:
```python
import jax
import jax.numpy as jnp
from jax import lax
from jax.sharding import PartitionSpec as P


def swapped(block, axis, stride):
    count = lax.axis_size(axis)
    route = []
    for low in range(count):
        high = low | 1 << stride
        if high != low and high < count:
            route += [(low, high), (high, low)]
    return lax.ppermute(block, axis, route)


def contract_rows(left, right):
    return lax.dot_general(
        left, right, (((0,), (0,)), ((), ())), preferred_element_type=jnp.float32
    )


def contract_cols(left, right):
    return lax.dot_general(
        left, right, (((1,), (1,)), ((), ())), preferred_element_type=jnp.float32
    )


def per_device(queries, key_rows, value_rows, out_grad, level_index, level_table):
    rows_here = queries.shape[0]
    columns = value_rows.shape[1]
    heads_here = level_table.shape[2]
    head_size = columns // heads_here
    table_rows = level_table.shape[1]
    tree_depth = lax.axis_size("seq").bit_length() - 1
    position = lax.axis_index("seq")
    matches = level_index[:, :, None] == jnp.arange(table_rows, dtype=jnp.int32)[None, None, :]
    weights = jnp.sum(jnp.where(matches[:, :, :, None], level_table[None], 0.0), axis=2)
    shaped = out_grad.astype(jnp.float32).reshape(rows_here, heads_here, head_size)

    def scale_by(height):
        return (
            (shaped * weights[:, height, :, None]).reshape(rows_here, columns).astype(jnp.bfloat16)
        )

    local_scaled = scale_by(0)
    scaled_list = [scale_by(height + 1) for height in range(tree_depth)]
    flags = [position >> height & 1 == 1 for height in range(tree_depth)]
    level_grads = []
    for height in range(tree_depth):
        product = contract_rows(queries, scaled_list[height])
        level_grads.append(jnp.where(flags[height], product, jnp.zeros_like(product)))
    block_state = contract_rows(key_rows, value_rows).astype(jnp.bfloat16)
    siblings = []
    block_sum = block_state
    for height in range(tree_depth):
        partner = swapped(block_sum, "seq", height)
        siblings.append(jnp.where(flags[height], partner, jnp.zeros_like(partner)))
        block_sum = (block_sum.astype(jnp.float32) + partner.astype(jnp.float32)).astype(
            jnp.bfloat16
        )
    pending = jnp.stack(level_grads)
    state_grad = jnp.zeros(block_state.shape, jnp.float32)
    for height in range(tree_depth):
        arrived = swapped(pending.astype(jnp.bfloat16), "seq", height).astype(pending.dtype)
        state_grad = state_grad + jnp.where(flags[height], jnp.zeros_like(arrived[0]), arrived[0])
        pending = pending[1:] + arrived[1:]
    row_ids = lax.broadcasted_iota(jnp.int32, (rows_here, rows_here), 0)
    col_ids = lax.broadcasted_iota(jnp.int32, (rows_here, rows_here), 1)
    causal = row_ids >= col_ids
    scores = contract_cols(queries, key_rows)
    masked = jnp.where(causal, scores, 0.0).astype(jnp.bfloat16)
    score_grad = jnp.where(causal, contract_cols(local_scaled, value_rows), 0.0).astype(
        jnp.bfloat16
    )
    state_low = state_grad.astype(jnp.bfloat16)
    value_grad = contract_rows(masked, local_scaled) + jnp.dot(
        key_rows, state_low, preferred_element_type=jnp.float32
    )
    query_grad = jnp.dot(score_grad, key_rows, preferred_element_type=jnp.float32)
    for height in range(tree_depth):
        query_grad = query_grad + contract_cols(scaled_list[height], siblings[height])
    key_grad = contract_rows(score_grad, queries) + contract_cols(value_rows, state_low)
    query_grad, key_grad = (
        lax.psum(query_grad.astype(jnp.bfloat16), "head").astype(jnp.float32),
        lax.psum(key_grad.astype(jnp.bfloat16), "head").astype(jnp.float32),
    )
    return (
        query_grad.astype(jnp.bfloat16),
        key_grad.astype(jnp.bfloat16),
        value_grad.astype(jnp.bfloat16),
    )


def solution(mesh):
    return jax.shard_map(
        per_device,
        mesh=mesh,
        in_specs=(
            P("seq", None),
            P("seq", None),
            P("seq", "head"),
            P("seq", "head"),
            P("seq", None),
            P(None, None, "head"),
        ),
        out_specs=(P("seq", None), P("seq", None), P("seq", "head")),
        check_vma=False,
    )
```

profile of v0, /device:TPU:6, one launch (start us, length us, event | category | flops | bytes accessed | tf_op | source)
XLA Modules:
  0.0 220.0 jit_solution(5472104066497696332)
XLA Ops:
  7.3 1.1 copy-done
  8.4 1.9 convolution_convert_fusion
  10.3 1.9 collective-permute-start
  12.3 0.5 copy.16
  12.9 0.3 select_reduce_fusion
  13.2 0.7 slice_bitcast_fusion.4
  13.9 2.8 %fusion.2 = (bf16[1024,512]{0,1:T(8,128)(2,1)S(1)}, bf16[1024,512]{0,1:T(8,128)(2,1)S(1)}, bf16[1024,512]{0,1:T(8,128)(2,1)S(1)}, bf16[1024,512]{0,1:T(8,128)(2,...) fusion(bf16[1024,512]{0,1:T(8,128)(2,1)S(1)} %copy.16, ...), kind=kLoop, calls=%fused_computation.12 | loop fusion | flops 7864320 | bytes 8617984 | tf_op jit(solution)/shard_map/convert_element_type | solution.py:43
  16.7 0.4 constant_dynamic-update-slice_fusion.4
  17.1 0.4 fusion.23
  17.6 0.4 constant_dynamic-update-slice_fusion.3
  18.1 0.4 constant_dynamic-update-slice_fusion.2
  18.6 0.4 constant_dynamic-update-slice_fusion.1
  19.1 0.4 constant_dynamic-update-slice_fusion
  19.5 2.4 %collective-permute-start.6 = (bf16[6,128,512]{1,2,0:T(8,128)(2,1)S(1)}, bf16[6,128,512]{1,2,0:T(8,128)(2,1)S(1)}, u32[]{:S(2)}, u32[]{:S(2)}) collective-permute-start(bf16[6,128,512]{1,2,0:T(8,128)(2,1)S(1)} %convert_dynamic-update-slice_fusion), channel_id=1, source_target_pairs={{0,8},{8,0},{16,24},{24,16},{32,40},{40,32},{48,56},{56,48},{64,72... | collective-permute-start | bytes 2359304 | tf_op jit(solution)/shard_map/ppermute | solution.py:14
  22.0 1.4 select_convert_fusion.1
  23.4 0.7 fusion.66
  24.1 0.7 fusion.67
  24.9 0.9 add_convert_fusion.4
  25.8 4.3 %collective-permute-start.1 = (bf16[128,512]{1,0:T(8,128)(2,1)S(1)}, bf16[128,512]{1,0:T(8,128)(2,1)S(1)}, u32[]{:S(2)}, u32[]{:S(2)}) collective-permute-start(bf16[128,512]{1,0:T(8,128)(2,1)S(1)} %add_convert_fusion.4), channel_id=1, source_target_pairs={{0,16},{16,0},{8,24},{24,8},{32,48},{48,32},{40,56},{56,40},{64,80... | collective-permute-start | bytes 393224 | tf_op jit(solution)/shard_map/ppermute | solution.py:14
  30.2 0.2 fusion.65
  30.4 1.9 collective-permute-start.7
  32.3 1.4 collective-permute-done.1
  33.8 6.1 %collective-permute-start.2 = (bf16[128,512]{1,0:T(8,128)(2,1)S(1)}, bf16[128,512]{1,0:T(8,128)(2,1)S(1)}, u32[]{:S(2)}, u32[]{:S(2)}) collective-permute-start(bf16[128,512]{1,0:T(8,128)(2,1)S(1)} %add_convert_fusion.3), channel_id=1, source_target_pairs={{0,32},{32,0},{8,40},{40,8},{16,48},{48,16},{24,56},{56,24},{64,96... | collective-permute-start | bytes 393224 | tf_op jit(solution)/shard_map/ppermute | solution.py:14
  39.9 0.5 convolution_add_fusion.1
  40.4 9.5 %collective-permute-done.2 = bf16[128,512]{1,0:T(8,128)(2,1)S(1)} collective-permute-done((bf16[128,512]{1,0:T(8,128)(2,1)S(1)}, bf16[128,512]{1,0:T(8,128)(2,1)S(1)}, u32[]{:S(2)}, u32[]{:S(2)}) %collective-permute-start.2) | collective-permute-done | bytes 131104 | tf_op jit(solution)/shard_map/ppermute | solution.py:14
  49.9 10.0 %collective-permute-start.3 = (bf16[128,512]{1,0:T(8,128)(2,1)S(1)}, bf16[128,512]{1,0:T(8,128)(2,1)S(1)}, u32[]{:S(2)}, u32[]{:S(2)}) collective-permute-start(bf16[128,512]{1,0:T(8,128)(2,1)S(1)} %add_convert_fusion.2), channel_id=1, source_target_pairs={{0,64},{64,0},{8,72},{72,8},{16,80},{80,16},{24,88},{88,24},{32,96... | collective-permute-start | bytes 393224 | tf_op jit(solution)/shard_map/ppermute | solution.py:14
  60.2 5.3 %collective-permute-start.8 = (bf16[4,128,512]{1,2,0:T(8,128)(2,1)S(1)}, bf16[4,128,512]{1,2,0:T(8,128)(2,1)S(1)}, u32[]{:S(2)}, u32[]{:S(2)}) collective-permute-start(bf16[4,128,512]{1,2,0:T(8,128)(2,1)S(1)} %get-tuple-element.9), channel_id=1, source_target_pairs={{0,32},{32,0},{8,40},{40,8},{16,48},{48,16},{24,56},{56,24},{64,96... | collective-permute-start | bytes 1572872 | tf_op jit(solution)/shard_map/ppermute | solution.py:14
  65.5 0.5 fusion.39
  66.0 2.7 %collective-permute-start.4 = (bf16[128,512]{1,0:T(8,128)(2,1)S(1)}, bf16[128,512]{1,0:T(8,128)(2,1)S(1)}, u32[]{:S(2)}, u32[]{:S(2)}) collective-permute-start(bf16[128,512]{1,0:T(8,128)(2,1)S(1)} %add_convert_fusion.1), channel_id=1, source_target_pairs={{0,128},{128,0},{8,136},{136,8},{16,144},{144,16},{24,152},{152,24... | collective-permute-start | bytes 393224 | tf_op jit(solution)/shard_map/ppermute | solution.py:14
  68.7 0.5 fusion.37
  69.2 21.5 %collective-permute-done.8 = bf16[4,128,512]{1,2,0:T(8,128)(2,1)S(1)} collective-permute-done((bf16[4,128,512]{1,2,0:T(8,128)(2,1)S(1)}, bf16[4,128,512]{1,2,0:T(8,128)(2,1)S(1)}, u32[]{:S(2)}, u32[]{:S(2)}) %collective-permute-start.8) | collective-permute-done | bytes 524320 | tf_op jit(solution)/shard_map/ppermute | solution.py:14
  90.8 0.2 fusion.63
  91.0 2.3 %collective-permute-start.9 = (bf16[3,128,512]{1,2,0:T(8,128)(2,1)S(1)}, bf16[3,128,512]{1,2,0:T(8,128)(2,1)S(1)}, u32[]{:S(2)}, u32[]{:S(2)}) collective-permute-start(bf16[3,128,512]{1,2,0:T(8,128)(2,1)S(1)} %get-tuple-element.7), channel_id=1, source_target_pairs={{0,64},{64,0},{8,72},{72,8},{16,80},{80,16},{24,88},{88,24},{32,96... | collective-permute-start | bytes 1179656 | tf_op jit(solution)/shard_map/ppermute | solution.py:14
  93.3 3.3 %collective-permute-start.5 = (bf16[128,512]{1,0:T(8,128)(2,1)S(1)}, bf16[128,512]{1,0:T(8,128)(2,1)S(1)}, u32[]{:S(2)}, u32[]{:S(2)}) collective-permute-start(bf16[128,512]{1,0:T(8,128)(2,1)S(1)} %add_convert_fusion), channel_id=1, source_target_pairs={{0,256},{256,0},{8,264},{264,8},{16,272},{272,16},{24,280},{280,24... | collective-permute-start | bytes 393224 | tf_op jit(solution)/shard_map/ppermute | solution.py:14
  96.7 0.5 fusion.35
  97.1 15.3 %collective-permute-done.9 = bf16[3,128,512]{1,2,0:T(8,128)(2,1)S(1)} collective-permute-done((bf16[3,128,512]{1,2,0:T(8,128)(2,1)S(1)}, bf16[3,128,512]{1,2,0:T(8,128)(2,1)S(1)}, u32[]{:S(2)}, u32[]{:S(2)}) %collective-permute-start.9) | collective-permute-done | bytes 393248 | tf_op jit(solution)/shard_map/ppermute | solution.py:14
  112.6 2.7 %collective-permute-start.10 = (bf16[2,128,512]{1,2,0:T(8,128)(2,1)S(1)}, bf16[2,128,512]{1,2,0:T(8,128)(2,1)S(1)}, u32[]{:S(2)}, u32[]{:S(2)}) collective-permute-start(bf16[2,128,512]{1,2,0:T(8,128)(2,1)S(1)} %get-tuple-element.5), channel_id=1, source_target_pairs={{0,128},{128,0},{8,136},{136,8},{16,144},{144,16},{24,152},{152,24... | collective-permute-start | bytes 786440 | tf_op jit(solution)/shard_map/ppermute | solution.py:14
  115.3 0.5 fusion.33
  115.8 5.1 %collective-permute-done.10 = bf16[2,128,512]{1,2,0:T(8,128)(2,1)S(1)} collective-permute-done((bf16[2,128,512]{1,2,0:T(8,128)(2,1)S(1)}, bf16[2,128,512]{1,2,0:T(8,128)(2,1)S(1)}, u32[]{:S(2)}, u32[]{:S(2)}) %collective-permute-start.10) | collective-permute-done | bytes 262176 | tf_op jit(solution)/shard_map/ppermute | solution.py:14
  120.9 4.3 %collective-permute-start.11 = (bf16[1,128,512]{1,2,0:T(8,128)(2,1)S(1)}, bf16[1,128,512]{1,2,0:T(8,128)(2,1)S(1)}, u32[]{:S(2)}, u32[]{:S(2)}) collective-permute-start(bf16[1,128,512]{1,2,0:T(8,128)(2,1)S(1)} %fusion.24), channel_id=1, source_target_pairs={{0,256},{256,0},{8,264},{264,8},{16,272},{272,16},{24,280},{280,24... | collective-permute-start | bytes 393224 | tf_op jit(solution)/shard_map/ppermute | solution.py:14
  125.3 1.2 fusion.14
  126.5 2.8 %collective-permute-done.11 = bf16[1,128,512]{1,2,0:T(8,128)(2,1)S(1)} collective-permute-done((bf16[1,128,512]{1,2,0:T(8,128)(2,1)S(1)}, bf16[1,128,512]{1,2,0:T(8,128)(2,1)S(1)}, u32[]{:S(2)}, u32[]{:S(2)}) %collective-permute-start.11) | collective-permute-done | bytes 131104 | tf_op jit(solution)/shard_map/ppermute | solution.py:14
  129.5 1.1 fusion.15
  130.6 3.1 %fusion.8 = f32[1024,512]{1,0:T(8,128)} fusion(bf16[1024,512]{0,1:T(8,128)(2,1)S(1)} %get-tuple-element.19, bf16[1024,128]{1,0:T(8,128)(2,1)S(1)} %copy-done.1, bf16[1024,128]{1,0:T(8,128)(2,1)S(1)} %copy-done.2), kind=kOutput, calls=%fused_computation.20 | convolution fusion | flops 1345323008 | bytes 3670016 | tf_op jit(solution)/shard_map/dot_general | solution.py:18
  133.8 3.0 %fusion.7 = bf16[1024,512]{1,0:T(8,128)(2,1)} fusion(f32[1024,512]{1,0:T(8,128)} %fusion.8, bf16[1024,128]{1,0:T(8,128)(2,1)S(1)} %copy-done.2, bf16[1,128,512]{1,2,0:T(8,128)(2,1)S(1)} %fusion.27), kind=kOutput, calls=%fused_computation.18 | convolution fusion | flops 135266304 | bytes 3538944 | tf_op jit(solution)/shard_map/dot_general | solution.py:77
  136.7 73.0 %all-reduce.3.cloned.1.call-done = (bf16[1024,128]{1,0:T(8,128)(2,1)}, bf16[1024,128]{1,0:T(8,128)(2,1)}) async-done(((bf16[1024,128]{1,0:T(8,128)(2,1)}, bf16[1024,128]{1,0:T(8,128)(2,1)}), (bf16[1024,128]{1,0:T(8,128)(2,1)}, bf16[1024,128]{1,0:T(8,128)(2,1)})) %all-reduce.3.cloned.1.call-update) | async-done | bytes 524304 | tf_op jit(solution)/shard_map/psum | solution.py:85
  209.8 1.7 copy.32
  211.5 1.7 copy.33
  (38 shorter events, 1.1 us)
Async XLA Ops:
  7.2 1.2 copy-start
  7.2 5.1 %copy-start.3 = (bf16[1024,512]{1,0:T(8,128)(2,1)S(1)}, bf16[1024,512]{1,0:T(8,128)(2,1)}, u32[]{:S(2)}) copy-start(bf16[1024,512]{1,0:T(8,128)(2,1)} %param.9) | copy-start | bytes 3145732
  7.2 5.6 %copy-start.4 = (s32[1024,7]{0,1:T(8,128)S(1)}, s32[1024,7]{0,1:T(8,128)}, u32[]{:S(2)}) copy-start(s32[1024,7]{0,1:T(8,128)} %param.10) | copy-start | bytes 86020
  7.2 5.7 %copy-start.5 = (f32[7,8,8]{2,1,0:T(8,128)S(1)}, f32[7,8,8]{2,1,0:T(8,128)}, u32[]{:S(2)}) copy-start(f32[7,8,8]{2,1,0:T(8,128)} %param.11) | copy-start | bytes 5380
  7.2 202.6 %all-reduce.3.cloned.1.call-start = ((), (), s32[]{:S(2)}) async-start(), calls=%async_computation | async-start | bytes 1048576 | tf_op jit(solution)/shard_map/psum | solution.py:85
  10.3 14.5 %collective-permute-start = (bf16[128,512]{1,0:T(8,128)(2,1)}, bf16[128,512]{1,0:T(8,128)(2,1)S(1)}, u32[]{:S(2)}, u32[]{:S(2)}) collective-permute-start(bf16[128,512]{1,0:T(8,128)(2,1)} %convolution_convert_fusion), channel_id=1, source_target_pairs={{0,8},{8,0},{16,24},{24,16},{32,40},{40,32},{48,56},{56,48},{64,72... | collective-permute-start | bytes 393224 | tf_op jit(solution)/shard_map/ppermute | solution.py:14
  13.9 2.8 %copy-start.1 = (bf16[1024,128]{1,0:T(8,128)(2,1)S(1)}, bf16[1024,128]{1,0:T(8,128)(2,1)}, u32[]{:S(2)}) copy-start(bf16[1024,128]{1,0:T(8,128)(2,1)} %param.6) | copy-start | bytes 786436
  19.5 10.6 %collective-permute-start.6 = (bf16[6,128,512]{1,2,0:T(8,128)(2,1)S(1)}, bf16[6,128,512]{1,2,0:T(8,128)(2,1)S(1)}, u32[]{:S(2)}, u32[]{:S(2)}) collective-permute-start(bf16[6,128,512]{1,2,0:T(8,128)(2,1)S(1)} %convert_dynamic-update-slice_fusion), channel_id=1, source_target_pairs={{0,8},{8,0},{16,24},{24,16},{32,40},{40,32},{48,56},{56,48},{64,72... | collective-permute-start | bytes 2359304 | tf_op jit(solution)/shard_map/ppermute | solution.py:14
  21.9 1.4 copy-start.2
  25.8 8.0 %collective-permute-start.1 = (bf16[128,512]{1,0:T(8,128)(2,1)S(1)}, bf16[128,512]{1,0:T(8,128)(2,1)S(1)}, u32[]{:S(2)}, u32[]{:S(2)}) collective-permute-start(bf16[128,512]{1,0:T(8,128)(2,1)S(1)} %add_convert_fusion.4), channel_id=1, source_target_pairs={{0,16},{16,0},{8,24},{24,8},{32,48},{48,32},{40,56},{56,40},{64,80... | collective-permute-start | bytes 393224 | tf_op jit(solution)/shard_map/ppermute | solution.py:14
  30.4 29.5 %collective-permute-start.7 = (bf16[5,128,512]{1,2,0:T(8,128)(2,1)S(1)}, bf16[5,128,512]{1,2,0:T(8,128)(2,1)S(1)}, u32[]{:S(2)}, u32[]{:S(2)}) collective-permute-start(bf16[5,128,512]{1,2,0:T(8,128)(2,1)S(1)} %get-tuple-element.11), channel_id=1, source_target_pairs={{0,16},{16,0},{8,24},{24,8},{32,48},{48,32},{40,56},{56,40},{64,80... | collective-permute-start | bytes 1966088 | tf_op jit(solution)/shard_map/ppermute | solution.py:14
  33.8 16.1 %collective-permute-start.2 = (bf16[128,512]{1,0:T(8,128)(2,1)S(1)}, bf16[128,512]{1,0:T(8,128)(2,1)S(1)}, u32[]{:S(2)}, u32[]{:S(2)}) collective-permute-start(bf16[128,512]{1,0:T(8,128)(2,1)S(1)} %add_convert_fusion.3), channel_id=1, source_target_pairs={{0,32},{32,0},{8,40},{40,8},{16,48},{48,16},{24,56},{56,24},{64,96... | collective-permute-start | bytes 393224 | tf_op jit(solution)/shard_map/ppermute | solution.py:14
  49.9 16.0 %collective-permute-start.3 = (bf16[128,512]{1,0:T(8,128)(2,1)S(1)}, bf16[128,512]{1,0:T(8,128)(2,1)S(1)}, u32[]{:S(2)}, u32[]{:S(2)}) collective-permute-start(bf16[128,512]{1,0:T(8,128)(2,1)S(1)} %add_convert_fusion.2), channel_id=1, source_target_pairs={{0,64},{64,0},{8,72},{72,8},{16,80},{80,16},{24,88},{88,24},{32,96... | collective-permute-start | bytes 393224 | tf_op jit(solution)/shard_map/ppermute | solution.py:14
  60.2 30.5 %collective-permute-start.8 = (bf16[4,128,512]{1,2,0:T(8,128)(2,1)S(1)}, bf16[4,128,512]{1,2,0:T(8,128)(2,1)S(1)}, u32[]{:S(2)}, u32[]{:S(2)}) collective-permute-start(bf16[4,128,512]{1,2,0:T(8,128)(2,1)S(1)} %get-tuple-element.9), channel_id=1, source_target_pairs={{0,32},{32,0},{8,40},{40,8},{16,48},{48,16},{24,56},{56,24},{64,96... | collective-permute-start | bytes 1572872 | tf_op jit(solution)/shard_map/ppermute | solution.py:14
  66.0 27.3 %collective-permute-start.4 = (bf16[128,512]{1,0:T(8,128)(2,1)S(1)}, bf16[128,512]{1,0:T(8,128)(2,1)S(1)}, u32[]{:S(2)}, u32[]{:S(2)}) collective-permute-start(bf16[128,512]{1,0:T(8,128)(2,1)S(1)} %add_convert_fusion.1), channel_id=1, source_target_pairs={{0,128},{128,0},{8,136},{136,8},{16,144},{144,16},{24,152},{152,24... | collective-permute-start | bytes 393224 | tf_op jit(solution)/shard_map/ppermute | solution.py:14
  91.0 21.5 %collective-permute-start.9 = (bf16[3,128,512]{1,2,0:T(8,128)(2,1)S(1)}, bf16[3,128,512]{1,2,0:T(8,128)(2,1)S(1)}, u32[]{:S(2)}, u32[]{:S(2)}) collective-permute-start(bf16[3,128,512]{1,2,0:T(8,128)(2,1)S(1)} %get-tuple-element.7), channel_id=1, source_target_pairs={{0,64},{64,0},{8,72},{72,8},{16,80},{80,16},{24,88},{88,24},{32,96... | collective-permute-start | bytes 1179656 | tf_op jit(solution)/shard_map/ppermute | solution.py:14
  93.3 22.0 %collective-permute-start.5 = (bf16[128,512]{1,0:T(8,128)(2,1)S(1)}, bf16[128,512]{1,0:T(8,128)(2,1)S(1)}, u32[]{:S(2)}, u32[]{:S(2)}) collective-permute-start(bf16[128,512]{1,0:T(8,128)(2,1)S(1)} %add_convert_fusion), channel_id=1, source_target_pairs={{0,256},{256,0},{8,264},{264,8},{16,272},{272,16},{24,280},{280,24... | collective-permute-start | bytes 393224 | tf_op jit(solution)/shard_map/ppermute | solution.py:14
  112.6 8.3 %collective-permute-start.10 = (bf16[2,128,512]{1,2,0:T(8,128)(2,1)S(1)}, bf16[2,128,512]{1,2,0:T(8,128)(2,1)S(1)}, u32[]{:S(2)}, u32[]{:S(2)}) collective-permute-start(bf16[2,128,512]{1,2,0:T(8,128)(2,1)S(1)} %get-tuple-element.5), channel_id=1, source_target_pairs={{0,128},{128,0},{8,136},{136,8},{16,144},{144,16},{24,152},{152,24... | collective-permute-start | bytes 786440 | tf_op jit(solution)/shard_map/ppermute | solution.py:14
  120.9 8.4 %collective-permute-start.11 = (bf16[1,128,512]{1,2,0:T(8,128)(2,1)S(1)}, bf16[1,128,512]{1,2,0:T(8,128)(2,1)S(1)}, u32[]{:S(2)}, u32[]{:S(2)}) collective-permute-start(bf16[1,128,512]{1,2,0:T(8,128)(2,1)S(1)} %fusion.24), channel_id=1, source_target_pairs={{0,256},{256,0},{8,264},{264,8},{16,272},{272,16},{24,280},{280,24... | collective-permute-start | bytes 393224 | tf_op jit(solution)/shard_map/ppermute | solution.py:14
Sparse Core Ops, SparseCore 0:
  130.7 79.0 all-reduce.2
where the time goes:
time: 221 us; the launch traced here: 220 us
  waiting for transfers between devices  129 us (58%)
  starting transfers between devices  47.4 us (21%)
  matrix products  18.3 us (8%)
  between operations  14.5 us (7%)
  local copies, waits for them, and re-layouts  5.83 us (3%)
  other arithmetic  5.31 us (2%)
    psum x1, waiting for transfers between devices, per_device(): lax.psum(query_grad.astype(jnp.bfloat16), 'head').astype(jnp.float32)  73 us
    ppermute x12, waiting for transfers between devices, swapped(): return lax.ppermute(block, axis, route)  55.6 us
    ppermute x12, starting transfers between devices, swapped(): return lax.ppermute(block, axis, route)  47.3 us
    dot_general x9, matrix products, contract_rows(): lax.dot_general(left, right, (((0,), (0,)), ((), ())), preferred_element_...  8.47 us
    dot_general x8, matrix products, contract_cols(): lax.dot_general(left, right, (((1,), (1,)), ((), ())), preferred_element_...  6.16 us
    unnamed x19, local copies, waits for them, and re-layouts  5.12 us
  transfers between devices with their start and end apart: 13, of which 7 were waited for; matrix products, arithmetic and copies ran while one was open for 10% of the time, Pallas kernels for 0%

commit v1 on v0

v1 whole, which is shorter than its diff:
```python
import jax
import jax.numpy as jnp
from jax import lax
from jax.experimental import pallas as pl
from jax.experimental.pallas import tpu as pltpu
from jax.sharding import PartitionSpec as P

MESH = pl.DeviceIdType.MESH
F32 = jnp.float32
BF16 = jnp.bfloat16

NX, NZ, NY = 4, 8, 8
LEVELS = 7
PICKS = 8
SLAB = 16
HALF = 256
TILE = 256


def rows_by_rows(left, right):
    return lax.dot_general(left, right, (((1,), (1,)), ((), ())), preferred_element_type=F32)


def cols_by_cols(left, right):
    return lax.dot_general(left, right, (((0,), (0,)), ((), ())), preferred_element_type=F32)


def plain(left, right):
    return lax.dot_general(left, right, (((1,), (0,)), ((), ())), preferred_element_type=F32)


def kernel(
    q_ref, k_ref, v_ref, og_ref, idx_ref, table_ref,
    qg_ref, kg_ref, vg_ref,
    scaled, picks_hi, q_turned, q_acc, k_acc, v_acc, vg_stage,
    b_own, b_both, a_slabs, t2_buf, t3_buf, t4_slots, t5_buf, sib,
    lg_own, lg_both, lg_sum, b_slabs, s_own, s_slots, g_buf, state,
    q_send_buf, k_send_buf, q_slots, k_slots, q_fin, k_fin,
    a0_s, a0_r, a1_s, a1_r, a2_s, a2_r, a3_s, a3_r, a4_s, a4_r,
    b0_s, b0_r, b1_s, b1_r, b2_s, b2_r, b3_s, b3_r, b4_s, b4_r,
    cq_s, cq_r, ck_s, ck_r, dq_s, dq_r, dk_s, dk_r, out_sem,
):
    seq = lax.axis_index("seq")
    y = lax.axis_index("head")
    core = lax.rem(seq, 2)
    other = 1 - core
    chip = lax.div(seq, 2)
    z = lax.rem(chip, NZ)
    x = lax.div(chip, NZ)
    tokens, columns = v_ref.shape

    def at(x_to, z_to, core_to):
        return ((x_to * NZ + z_to) * 2 + core_to, y)

    def z_at(step):
        return lax.rem(z + step, NZ)

    def x_at(step):
        return lax.rem(x + step, NX)

    def y_at(step):
        return lax.rem(y + step, NY)

    def send(src, dst, s_sem, r_sem, to):
        return pltpu.make_async_remote_copy(
            src_ref=src, dst_ref=dst, send_sem=s_sem, recv_sem=r_sem,
            device_id=to, device_id_type=MESH,
        )

    peer = at(x, z, other)
    z_order = [1, 7, 2, 6, 3, 5, 4]

    barrier = pltpu.get_barrier_semaphore()
    pl.semaphore_signal(barrier, inc=1, device_id=peer, device_id_type=MESH)
    for step in range(1, NZ):
        pl.semaphore_signal(barrier, inc=1, device_id=at(x, z_at(step), core), device_id_type=MESH)
    for step in range(1, NX):
        pl.semaphore_signal(barrier, inc=1, device_id=at(x_at(step), z, core), device_id_type=MESH)
    for step in range(1, NY):
        pl.semaphore_signal(barrier, inc=1, device_id=(seq, y_at(step)), device_id_type=MESH)

    block_state = cols_by_cols(k_ref[...], v_ref[...]).astype(BF16)
    for half in range(2):
        b_own[half] = block_state[:, half * HALF:(half + 1) * HALF].reshape(NZ, SLAB, HALF)
    pl.semaphore_wait(barrier, 1 + (NZ - 1) + (NX - 1) + (NY - 1))
    a0 = send(b_own, b_both, a0_s, a0_r, peer)
    a0.start()

    head_of = lax.broadcasted_iota(jnp.int32, (PICKS, columns), 1) // (columns // table_ref.shape[2])
    for level in range(LEVELS):
        wide = jnp.zeros((PICKS, columns), F32)
        for head in range(table_ref.shape[2]):
            wide = jnp.where(head_of == head, table_ref[level, :, head:head + 1], wide)
        high = wide.astype(BF16)
        low = (wide - high.astype(F32)).astype(BF16)
        picks_hi[level] = jnp.concatenate([high.astype(F32), low.astype(F32)], axis=0).astype(BF16)
    q_turned[...] = q_ref[...].T

    pick_of = lax.rem(lax.broadcasted_iota(jnp.int32, (2 * PICKS, tokens), 0), PICKS)

    def scale_level(level):
        chosen = (pick_of == idx_ref[level]).astype(F32).astype(BF16)
        for tile in range(tokens // TILE):
            rows = slice(tile * TILE, (tile + 1) * TILE)
            weight = cols_by_cols(chosen[:, rows], picks_hi[level])
            scaled[level, rows, :] = (og_ref[rows, :].astype(F32) * weight).astype(BF16)

    def flag(level):
        span = 2 ** (level - 1)
        return lax.rem(lax.div(seq, span), 2) == 1

    def level_grad(level):
        product = plain(q_turned[...], scaled[level]).astype(BF16)
        for half in range(2):
            lg_own[level, half] = product[:, half * HALF:(half + 1) * HALF].reshape(NZ, SLAB, HALF)

    def b0_copy(level):
        return send(lg_own.at[level, other], lg_both.at[level], b0_s.at[level], b0_r.at[level], peer)

    def b0_low():
        return send(lg_own.at[1], state, b0_s.at[1], b0_r.at[1], peer)

    def a1_copy(step):
        zt = z_at(step)
        return send(lg_sum.at[0, zt], a_slabs.at[z], a1_s.at[step], a1_r.at[z], at(x, zt, core))

    def a1_wait(step):
        zf = z_at(step)
        return send(lg_sum.at[0, zf], a_slabs.at[zf], a1_s.at[step], a1_r.at[zf], at(x, zf, core))

    def level_pass(level):
        scale_level(level)
        level_grad(level)

    def levels_loop(first, last):
        def body(level, span):
            level_pass(level)

            @pl.when(lax.rem(lax.div(seq, span), 2) == 1)
            def _():
                b0_copy(level).start()

            return span * 2

        lax.fori_loop(first, last, body, jnp.int32(2 ** (first - 1)))

    levels_loop(6, 7)

    a0.wait_recv()
    lg_sum[0] = (b_own[core].astype(F32) + b_both[core].astype(F32)).astype(BF16)
    for step in z_order:
        a1_copy(step).start()
    a_slabs[z] = lg_sum[0, z]

    levels_loop(2, 6)

    level_pass(1)

    @pl.when(core == 1)
    def _():
        b0_low().start()

    def b1_copy(level, step):
        zt = z_at(step)
        return send(
            lg_sum.at[level, zt], b_slabs.at[level, z], b1_s.at[level, step],
            b1_r.at[level, z], at(x, zt, core),
        )

    def b1_wait(level, zf):
        return send(
            lg_sum.at[level, zf], b_slabs.at[level, zf], b1_s.at[level, 0],
            b1_r.at[level, zf], at(x, zf, core),
        )

    for level in (6, 5, 4, 3, 2):
        @pl.when(flag(level))
        def _(level=level):
            b0_copy(level).wait_recv()
            lg_sum[level] = (lg_own[level, core].astype(F32) + lg_both[level].astype(F32)).astype(BF16)
            for step in z_order:
                b1_copy(level, step).start()
            b_slabs[level, z] = lg_sum[level, z]

    scale_level(0)

    for step in z_order:
        a1_wait(step).wait_recv()
    tier1 = [a_slabs[i].astype(F32) for i in range(NZ)]
    tier2 = [(tier1[2 * i] + tier1[2 * i + 1]).astype(BF16) for i in range(4)]
    tier3 = [(tier2[2 * i].astype(F32) + tier2[2 * i + 1].astype(F32)).astype(BF16) for i in range(2)]
    tier4 = (tier3[0].astype(F32) + tier3[1].astype(F32)).astype(BF16)
    for i in range(4):
        t2_buf[i] = tier2[i]
    t3_buf[...] = tier3[0]
    t4_slots[x] = tier4

    def a2_copy(step):
        xt = x_at(step)
        return send(t4_slots.at[x], t4_slots.at[x], a2_s.at[step], a2_r.at[x], at(xt, z, core))

    def a2_wait(step):
        xf = x_at(step)
        return send(t4_slots.at[xf], t4_slots.at[xf], a2_s.at[step], a2_r.at[xf], at(xf, z, core))

    for step in range(1, NX):
        a2_copy(step).start()

    def a3_src(level, zt):
        if level == 2:
            return a_slabs.at[zt - 1]
        if level == 3:
            return t2_buf.at[lax.div(zt, 2) - 1]
        if level == 4:
            return t3_buf
        if level == 5:
            return t4_slots.at[x - 1]
        return t5_buf

    def reads(level, zt):
        if level == 5:
            return lax.rem(x, 2) == 1
        if level == 6:
            return lax.div(x, 2) == 1
        return lax.rem(lax.div(zt, 2 ** (level - 2)), 2) == 1

    def a3_copy(level, step):
        zt = z_at(step)
        return send(
            a3_src(level, zt), sib.at[level, core, z], a3_s.at[level, step],
            a3_r.at[level, z], at(x, zt, core),
        )

    def a3_wait(level, step):
        zf = z_at(step)
        return send(
            sib.at[level, core, zf], sib.at[level, core, zf], a3_s.at[level, step],
            a3_r.at[level, zf], at(x, zf, core),
        )

    def a3_own(level):
        @pl.when(reads(level, z))
        def _():
            sib[level, core, z] = a3_src(level, z)[...]

    for step in z_order:
        for level in (4, 3, 2):
            @pl.when(reads(level, z_at(step)))
            def _(level=level, step=step):
                a3_copy(level, step).start()
    for level in (4, 3, 2):
        a3_own(level)

    def causal(first):
        count = tokens - first * TILE
        row = lax.broadcasted_iota(jnp.int32, (TILE, count), 0)
        col = lax.broadcasted_iota(jnp.int32, (TILE, count), 1)
        return col >= row

    def block_tile(j):
        rows = slice(j * TILE, (j + 1) * TILE)
        later = slice(j * TILE, tokens)
        keep = causal(j)
        masked_t = jnp.where(keep, rows_by_rows(k_ref[rows, :], q_ref[later, :]), 0.0).astype(BF16)
        v_acc[rows, :] = plain(masked_t, scaled[0, later, :])
        grad_t = jnp.where(keep, rows_by_rows(v_ref[rows, :], scaled[0, later, :]), 0.0).astype(BF16)
        k_acc[rows, :] = plain(grad_t, q_ref[later, :])
        term = cols_by_cols(grad_t, k_ref[rows, :])
        if j == 0:
            q_acc[...] = term
        else:
            q_acc[later, :] += term

    block_tile(0)

    for step in range(1, NX):
        a2_wait(step).wait_recv()
    t5_buf[...] = (t4_slots[0].astype(F32) + t4_slots[1].astype(F32)).astype(BF16)
    for level in (5, 6):
        @pl.when(reads(level, z))
        def _(level=level):
            for step in z_order:
                a3_copy(level, step).start()
        a3_own(level)

    for level, sources in ((2, (1, 3, 5, 7)), (3, (2, 3, 6, 7)), (4, (4, 5, 6, 7))):
        for zf in sources:
            @pl.when(z != zf)
            def _(level=level, zf=zf):
                b1_wait(level, zf).wait_recv()

    def b2_five():
        return send(s_own.at[0], s_slots.at[0], b2_s.at[0], b2_r.at[0], at(x - 1, z, core))

    def b2_six(target):
        return send(s_own.at[1], s_slots.at[x - 1], b2_s.at[1 + target], b2_r.at[x - 1], at(target, z, core))

    def b2_wait(slot, xf):
        return send(s_slots.at[slot], s_slots.at[slot], b2_s.at[slot], b2_r.at[slot], at(xf, z, core))

    def slab_sum(level):
        total = b_slabs[level, 0].astype(F32)
        for i in range(1, NZ):
            total += b_slabs[level, i].astype(F32)
        return total.astype(BF16)

    for level in (6, 5):
        @pl.when(flag(level))
        def _(level=level):
            for step in z_order:
                b1_wait(level, z_at(step)).wait_recv()
            s_own[level - 5] = slab_sum(level)
            if level == 6:
                b2_six(0).start()
                b2_six(1).start()
            else:
                b2_five().start()

    block_tile(1)

    @pl.when(lax.rem(x, 2) == 0)
    def _():
        b2_wait(0, x + 1).wait_recv()

    @pl.when(lax.div(x, 2) == 0)
    def _():
        b2_wait(1, 2).wait_recv()
        b2_wait(2, 3).wait_recv()

    zero = jnp.zeros((SLAB, HALF), F32)
    far = jnp.where(lax.rem(x, 2) == 0, s_slots[0].astype(F32), zero)
    far += jnp.where(lax.div(x, 2) == 0, s_slots[1].astype(F32) + s_slots[2].astype(F32), zero)
    upper = b_slabs[4, 4].astype(F32)
    for i in (5, 6, 7):
        upper += b_slabs[4, i].astype(F32)
    for zt in range(NZ):
        total = far
        if zt < 4:
            total = total + upper
        if zt % 4 < 2:
            base = zt - zt % 4
            total = total + b_slabs[3, base + 2].astype(F32) + b_slabs[3, base + 3].astype(F32)
        if zt % 2 == 0:
            total = total + b_slabs[2, zt + 1].astype(F32)
        s_own[2 + zt] = total.astype(BF16)

    def b3_copy(step):
        zt = z_at(step)
        return send(s_own.at[2 + zt], g_buf.at[core, z], b3_s.at[step], b3_r.at[z], at(x, zt, core))

    def b3_wait(step):
        zf = z_at(step)
        return send(g_buf.at[core, zf], g_buf.at[core, zf], b3_s.at[step], b3_r.at[zf], at(x, zf, core))

    for step in z_order:
        b3_copy(step).start()
    g_buf[core, z] = s_own[2 + z]

    block_tile(2)
    block_tile(3)

    def a4_copy(level):
        return send(sib.at[level, core], sib.at[level, core], a4_s.at[level], a4_r.at[level], peer)

    def a4_wait(level):
        return send(sib.at[level, other], sib.at[level, other], a4_s.at[level], a4_r.at[level], peer)

    for level in (2, 3, 4, 5, 6):
        @pl.when(reads(level, z))
        def _(level=level):
            for step in z_order:
                a3_wait(level, step).wait_recv()
            a4_copy(level).start()

    def add_sibling(level, halves):
        for half in range(2):
            block = halves(half).reshape(NZ * SLAB, HALF)
            q_acc[...] += rows_by_rows(scaled[level, :, half * HALF:(half + 1) * HALF], block)

    @pl.when(core == 1)
    def _():
        add_sibling(1, lambda half: b_both[half])

    for level in (2, 3, 4, 5, 6):
        @pl.when(reads(level, z))
        def _(level=level):
            a4_wait(level).wait_recv()
            add_sibling(level, lambda half: sib[level, half])

    def c_copy(buf, slots, s_sem, r_sem, step):
        yt = y_at(step)
        return send(buf.at[yt], slots.at[y], s_sem.at[step], r_sem.at[y], (seq, yt))

    def c_wait(buf, slots, s_sem, r_sem, step):
        yf = y_at(step)
        return send(buf.at[yf], slots.at[yf], s_sem.at[step], r_sem.at[yf], (seq, yf))

    def c_start(acc, buf, slots, s_sem, r_sem):
        buf[...] = acc[...].astype(BF16).reshape(buf.shape)
        for step in z_order:
            c_copy(buf, slots, s_sem, r_sem, step).start()
        slots[y] = buf[y]

    c_start(q_acc, q_send_buf, q_slots, cq_s, cq_r)

    for step in z_order:
        b3_wait(step).wait_recv()

    def b4_copy():
        return send(g_buf.at[core], g_buf.at[core], b4_s, b4_r, peer)

    def b4_wait():
        return send(g_buf.at[other], g_buf.at[other], b4_s, b4_r, peer)

    b4_copy().start()

    @pl.when(core == 0)
    def _():
        b0_low().wait_recv()

    b4_wait().wait_recv()
    near = jnp.where(core == 0, state[...].astype(F32), 0.0)
    low = (near + g_buf[...].astype(F32)).astype(BF16).reshape(2, NZ * SLAB, HALF)
    for half in range(2):
        k_acc[...] += rows_by_rows(v_ref[:, half * HALF:(half + 1) * HALF], low[half])
    c_start(k_acc, k_send_buf, k_slots, ck_s, ck_r)

    for half in range(2):
        cols = slice(half * HALF, (half + 1) * HALF)
        vg_stage[:, cols] = (v_acc[:, cols] + plain(k_ref[...], low[half])).astype(BF16)
    out_copy = pltpu.make_async_copy(vg_stage, vg_ref, out_sem.at[0])
    out_copy.start()

    def d_copy(fin, out, s_sem, r_sem, step):
        yt = y_at(step)
        return send(fin, out.at[y], s_sem.at[step], r_sem.at[y], (seq, yt))

    def d_wait(fin, out, s_sem, r_sem, step):
        yf = y_at(step)
        return send(fin, out.at[yf], s_sem.at[step], r_sem.at[yf], (seq, yf))

    def finish(buf, slots, fin, out, s_sem, r_sem, s_out, r_out, own_sem):
        for step in z_order:
            c_wait(buf, slots, s_sem, r_sem, step).wait_recv()
        total = slots[0].astype(F32)
        for i in range(1, NY):
            total += slots[i].astype(F32)
        fin[...] = total.astype(BF16)
        for step in z_order:
            d_copy(fin, out, s_out, r_out, step).start()
        own = pltpu.make_async_copy(fin, out.at[y], own_sem)
        own.start()
        return own

    q_own = finish(q_send_buf, q_slots, q_fin, qg_ref, cq_s, cq_r, dq_s, dq_r, out_sem.at[1])
    k_own = finish(k_send_buf, k_slots, k_fin, kg_ref, ck_s, ck_r, dk_s, dk_r, out_sem.at[2])

    a0.wait_send()
    for step in z_order:
        a1_copy(step).wait_send()
        b3_copy(step).wait_send()
        for level in (2, 3, 4, 5, 6):
            @pl.when(flag(level))
            def _(level=level, step=step):
                b1_copy(level, step).wait_send()

            @pl.when(reads(level, z_at(step)))
            def _(level=level, step=step):
                a3_copy(level, step).wait_send()
    for step in range(1, NX):
        a2_copy(step).wait_send()
    for level in (2, 3, 4, 5, 6):
        @pl.when(flag(level))
        def _(level=level):
            b0_copy(level).wait_send()
            a4_copy(level).wait_send()

    @pl.when(core == 1)
    def _():
        b0_low().wait_send()

    @pl.when(lax.rem(x, 2) == 1)
    def _():
        b2_five().wait_send()

    @pl.when(lax.div(x, 2) == 1)
    def _():
        b2_six(0).wait_send()
        b2_six(1).wait_send()

    b4_copy().wait_send()
    for step in z_order:
        c_copy(q_send_buf, q_slots, cq_s, cq_r, step).wait_send()
        c_copy(k_send_buf, k_slots, ck_s, ck_r, step).wait_send()
    for step in z_order:
        d_wait(q_fin, qg_ref, dq_s, dq_r, step).wait_recv()
        d_wait(k_fin, kg_ref, dk_s, dk_r, step).wait_recv()
        d_copy(q_fin, qg_ref, dq_s, dq_r, step).wait_send()
        d_copy(k_fin, kg_ref, dk_s, dk_r, step).wait_send()
    q_own.wait()
    k_own.wait()
    out_copy.wait()


def per_device(queries, key_rows, value_rows, out_grad, level_index, level_table):
    tokens, state_size = queries.shape
    columns = value_rows.shape[1]
    index_rows = level_index.T.reshape(LEVELS, 1, tokens)
    vmem = pl.BlockSpec(memory_space=pltpu.VMEM)
    anywhere = pl.BlockSpec(memory_space=pl.ANY)
    dma = pltpu.SemaphoreType.DMA
    half = (NZ, SLAB, HALF)
    rows_out = tokens // NY
    slots = (NY, rows_out, state_size)
    scratch = [
        pltpu.VMEM((LEVELS, tokens, columns), BF16),
        pltpu.VMEM((LEVELS, 2 * PICKS, columns), BF16),
        pltpu.VMEM((state_size, tokens), BF16),
        pltpu.VMEM((tokens, state_size), F32),
        pltpu.VMEM((tokens, state_size), F32),
        pltpu.VMEM((tokens, columns), F32),
        pltpu.VMEM((tokens, columns), BF16),
        pltpu.VMEM((2,) + half, BF16),
        pltpu.VMEM((2,) + half, BF16),
        pltpu.VMEM(half, BF16),
        pltpu.VMEM((4, SLAB, HALF), BF16),
        pltpu.VMEM((SLAB, HALF), BF16),
        pltpu.VMEM((NX, SLAB, HALF), BF16),
        pltpu.VMEM((SLAB, HALF), BF16),
        pltpu.VMEM((LEVELS, 2) + half, BF16),
        pltpu.VMEM((LEVELS, 2) + half, BF16),
        pltpu.VMEM((LEVELS,) + half, BF16),
        pltpu.VMEM((LEVELS,) + half, BF16),
        pltpu.VMEM((LEVELS,) + half, BF16),
        pltpu.VMEM((2 + NZ, SLAB, HALF), BF16),
        pltpu.VMEM((3, SLAB, HALF), BF16),
        pltpu.VMEM((2,) + half, BF16),
        pltpu.VMEM((2,) + half, BF16),
        pltpu.VMEM(slots, BF16),
        pltpu.VMEM(slots, BF16),
        pltpu.VMEM(slots, BF16),
        pltpu.VMEM(slots, BF16),
        pltpu.VMEM(slots[1:], BF16),
        pltpu.VMEM(slots[1:], BF16),
        dma, dma, dma((NZ,)), dma((NZ,)), dma((NX,)), dma((NX,)),
        dma((LEVELS, NZ)), dma((LEVELS, NZ)), dma((LEVELS,)), dma((LEVELS,)),
        dma((LEVELS,)), dma((LEVELS,)), dma((LEVELS, NZ)), dma((LEVELS, NZ)),
        dma((3,)), dma((3,)), dma((NZ,)), dma((NZ,)), dma, dma,
        dma((NY,)), dma((NY,)), dma((NY,)), dma((NY,)),
        dma((NY,)), dma((NY,)), dma((NY,)), dma((NY,)), dma((3,)),
    ]
    query_grad, key_grad, value_grad = pl.pallas_call(
        kernel,
        out_shape=(
            jax.ShapeDtypeStruct(slots, BF16),
            jax.ShapeDtypeStruct(slots, BF16),
            jax.ShapeDtypeStruct((tokens, columns), BF16),
        ),
        in_specs=[vmem] * 6,
        out_specs=(anywhere, anywhere, anywhere),
        scratch_shapes=scratch,
        compiler_params=pltpu.CompilerParams(
            collective_id=0, has_side_effects=True, vmem_limit_bytes=60 * 1024 * 1024
        ),
        name="fenwick_backward",
    )(queries, key_rows, value_rows, out_grad, index_rows, level_table)
    return (
        query_grad.reshape(tokens, state_size),
        key_grad.reshape(tokens, state_size),
        value_grad,
    )


def solution(mesh):
    return jax.shard_map(
        per_device,
        mesh=mesh,
        in_specs=(
            P("seq", None),
            P("seq", None),
            P("seq", "head"),
            P("seq", "head"),
            P("seq", None),
            P(None, None, "head"),
        ),
        out_specs=(P("seq", None), P("seq", None), P("seq", "head")),
        check_vma=False,
    )
```

time: 221 us -> 70.4 us (0.32)
  waiting for transfers between devices: 129 us -> 0 us
  Pallas kernels: 0 us -> 62.8 us
  starting transfers between devices: 47.4 us -> 0 us
  matrix products: 18.3 us -> 0 us
  between operations: 14.5 us -> 0.65 us
  other arithmetic: 5.31 us -> 0 us
    psum x1 -> x0, waiting for transfers between devices: 73 us -> none  [per_device(): lax.psum(query_grad.astype(jnp.bfloat16), 'head').astype(jnp.float32)]
    pallas_call x0 -> x1, Pallas kernels: none -> 62.8 us  [per_device(): pl.pallas_call(kernel, out_shape=(jax.ShapeDtypeStruct(slots, BF16), jax....]
    ppermute x12 -> x0, waiting for transfers between devices: 55.6 us -> none  [swapped(): return lax.ppermute(block, axis, route)]
    ppermute x12 -> x0, starting transfers between devices: 47.3 us -> none  [swapped(): return lax.ppermute(block, axis, route)]
    dot_general x19 -> x0, matrix products: 18.3 us -> none  [the longest x9 8.47 us: contract_rows(): lax.dot_general(left, right, (((0,), (0,)), ((), ())), preferred_element_...]
    convert_element_type x17 -> x0, other arithmetic: 4.95 us -> none  [the longest x1 2.79 us: scale_by(): (shaped * weights[:, height, :, None]).reshape(rows_here, columns)]
    unnamed x19 -> x5, local copies, waits for them, and re-layouts: 5.12 us -> 4.4 us
  transfers between devices with their start and end apart: 13 -> 0, of which waited for: 7 -> 0; matrix products, arithmetic and copies ran while one was open for 10% -> 0% of each run, Pallas kernels for 0% -> 0%
where the time goes in v1:
time: 70.4 us; the launch traced here: 69.2 us
  Pallas kernels  62.8 us (89%)
  local copies, waits for them, and re-layouts  5.79 us (8%)
    pallas_call x1, Pallas kernels, per_device(): pl.pallas_call(kernel, out_shape=(jax.ShapeDtypeStruct(slots, BF16), jax....  62.8 us
    unnamed x5, local copies, waits for them, and re-layouts  4.4 us

profile of v1, /device:TPU:6, one launch (start us, length us, event | category | flops | bytes accessed | tf_op | source)
XLA Modules:
  0.0 69.2 jit_solution(2120941186007872935)
XLA Ops:
  0.6 1.4 %reshape.15.idx_ref = s32[7,1,1024]{2,1,0:T(1,128)} reshape(s32[7,1024]{1,0:T(8,128)} %bitcast.5) | data formatting | bytes 57344 | tf_op jit(solution)/shard_map/reshape | solution.py:508
  2.0 62.8 %fenwick_backward.1 = (bf16[8,128,128]{2,1,0:T(8,128)(2,1)}, bf16[8,128,128]{2,1,0:T(8,128)(2,1)}, bf16[1024,512]{1,0:T(8,128)(2,1)}) custom-call(bf16[1024,128]{1,0:T(8,128)(2,1)} %q_ref.1, bf16[1024,128]{1,0:T(8,128)(2,1)} %k_ref.1, bf16[1024,512]{1,0:T(8,128)(2,1)} %v_ref.1, bf16[1024,512]{1,0:T(8,128)(2,1)} %og_ref.1, s32[7,1,1024]{2,1,0:T(1,128)} %reshape.15.idx_ref, ...), custom_call_target="tpu_custom_call" | custom-call | tf_op jit(solution)/shard_map/fenwick_backward/pallas_call | solution.py:552
  64.8 0.0 copy-start
  64.8 1.8 %copy.12 = bf16[1024,128]{1,0:T(8,128)(2,1)} copy(bf16[1024,128]{1,0:T(8,128)(2,1)} %bitcast.4) | data formatting | bytes 524288
  66.6 1.7 %copy.13 = bf16[1024,128]{1,0:T(8,128)(2,1)} copy(bf16[1024,128]{1,0:T(8,128)(2,1)} %bitcast.3) | data formatting | bytes 524288
  68.3 0.0 copy-done
  68.3 1.0 %copy.14 = bf16[1024,512]{1,0:T(8,128)(2,1)} copy(bf16[1024,512]{1,0:T(8,128)(2,1)S(1)} %copy-done) | data formatting | bytes 2097152
Async XLA Ops:
  64.8 3.4 %copy-start = (bf16[1024,512]{1,0:T(8,128)(2,1)S(1)}, bf16[1024,512]{1,0:T(8,128)(2,1)}, u32[]{:S(2)}) copy-start(bf16[1024,512]{1,0:T(8,128)(2,1)} %get-tuple-element.14) | copy-start | bytes 3145732

commit v2 on v0

v2 whole, which is shorter than its diff:
```python
import jax
import jax.numpy as jnp
from jax import lax
from jax.experimental import pallas as pl
from jax.experimental.pallas import tpu as pltpu
from jax.sharding import PartitionSpec as P

MESH = pl.DeviceIdType.MESH
F32 = jnp.float32
BF16 = jnp.bfloat16

NX, NZ, NY = 4, 8, 8
LEVELS = 7
PICKS = 8
SLAB = 16
HALF = 256
TILE = 256


def rows_by_rows(left, right):
    return lax.dot_general(left, right, (((1,), (1,)), ((), ())), preferred_element_type=F32)


def cols_by_cols(left, right):
    return lax.dot_general(left, right, (((0,), (0,)), ((), ())), preferred_element_type=F32)


def plain(left, right):
    return lax.dot_general(left, right, (((1,), (0,)), ((), ())), preferred_element_type=F32)


def kernel(
    q_in, k_in, v_in, og_in, idx_in, table_in,
    qg_ref, kg_ref, vg_ref,
    q_ref, k_ref, v_ref, og_ref, idx_ref, table_ref,
    scaled, picks, q_turned, q_acc, k_acc, v_acc,
    b_own, b_both, a_slabs, t2_buf, t3_buf, t4_slots, t5_buf, sib,
    lg_own, lg_both, lg_sum, b_slabs, s_own, s_slots, g_buf, state,
    q_part, k_part, q_relay, k_relay, q_slots, k_slots,
    in_sem, tree_s, head_s, level_s,
    a0_r, a1_r, a2_r, a3_r, a4_r, b0_r, b1_r, b2_r, b3_r, b4_r, q_r, k_r,
):
    seq = lax.axis_index("seq")
    y = lax.axis_index("head")
    core = lax.rem(seq, 2)
    other = 1 - core
    chip = lax.div(seq, 2)
    z = lax.rem(chip, NZ)
    x = lax.div(chip, NZ)
    tokens, columns = v_ref.shape

    def at(x_to, z_to, core_to):
        return ((x_to * NZ + z_to) * 2 + core_to, y)

    def z_at(step):
        return lax.rem(z + step, NZ)

    def x_at(step):
        return lax.rem(x + step, NX)

    turn = 1 - 2 * core

    def y_at(step):
        return lax.rem(y + step * turn + NY, NY)

    def send(src, dst, s_sem, r_sem, to):
        pltpu.make_async_remote_copy(
            src_ref=src, dst_ref=dst, send_sem=s_sem, recv_sem=r_sem,
            device_id=to, device_id_type=MESH,
        ).start()

    peer = at(x, z, other)

    def arrived(like, r_sem):
        pltpu.make_async_remote_copy(
            src_ref=like, dst_ref=like, send_sem=tree_s, recv_sem=r_sem,
            device_id=peer, device_id_type=MESH,
        ).wait_recv()

    def sent(kib, s_sem):
        like = scaled.at[0, pl.ds(0, kib)]
        pltpu.make_async_remote_copy(
            src_ref=like, dst_ref=like, send_sem=s_sem, recv_sem=a0_r,
            device_id=peer, device_id_type=MESH,
        ).wait_send()

    z_order = [1, 7, 2, 6, 3, 5, 4]

    barrier = pltpu.get_barrier_semaphore()
    for step in range(1, NZ):
        pl.semaphore_signal(barrier, inc=1, device_id=at(x, z_at(step), core), device_id_type=MESH)
    for step in range(1, NX):
        pl.semaphore_signal(barrier, inc=1, device_id=at(x_at(step), z, core), device_id_type=MESH)
    for step in (2, -2, 1, -1):
        pl.semaphore_signal(barrier, inc=1, device_id=(seq, y_at(step)), device_id_type=MESH)
    pl.semaphore_signal(barrier, inc=1, device_id=peer, device_id_type=MESH)

    loads = [
        pltpu.make_async_copy(src, dst, in_sem.at[i])
        for i, (src, dst) in enumerate((
            (k_in, k_ref), (v_in, v_ref), (table_in, table_ref),
            (idx_in, idx_ref), (og_in, og_ref), (q_in, q_ref),
        ))
    ]
    for load in loads:
        load.start()

    loads[0].wait()
    loads[1].wait()
    block_state = cols_by_cols(k_ref[...], v_ref[...]).astype(BF16)
    for half in range(2):
        b_own[half] = block_state[:, half * HALF:(half + 1) * HALF].reshape(NZ, SLAB, HALF)

    loads[2].wait()
    head_of = lax.broadcasted_iota(jnp.int32, (PICKS, columns), 1) // (columns // table_ref.shape[2])
    for level in range(LEVELS):
        wide = jnp.zeros((PICKS, columns), F32)
        for head in range(table_ref.shape[2]):
            wide = jnp.where(head_of == head, table_ref[level, :, head:head + 1], wide)
        high = wide.astype(BF16)
        low = (wide - high.astype(F32)).astype(BF16)
        picks[level] = jnp.concatenate([high.astype(F32), low.astype(F32)], axis=0).astype(BF16)
    for load in loads[3:]:
        load.wait()
    q_turned[...] = q_ref[...].T

    pick_of = lax.rem(lax.broadcasted_iota(jnp.int32, (2 * PICKS, tokens), 0), PICKS)

    def scale_level(level):
        chosen = (pick_of == idx_ref[level:level + 1, :]).astype(F32).astype(BF16)
        for tile in range(tokens // TILE):
            rows = slice(tile * TILE, (tile + 1) * TILE)
            weight = cols_by_cols(chosen[:, rows], picks[level])
            scaled[level, rows, :] = (og_ref[rows, :].astype(F32) * weight).astype(BF16)

    def flag(level):
        return lax.rem(lax.div(seq, 2 ** (level - 1)), 2) == 1

    for level in range(6, 0, -1):
        scale_level(level)
        product = plain(q_turned[...], scaled[level]).astype(BF16)
        for half in range(2):
            lg_own[level, half] = product[:, half * HALF:(half + 1) * HALF].reshape(NZ, SLAB, HALF)

    pl.semaphore_wait(barrier, 1 + (NZ - 1) + (NX - 1) + 4)

    send(b_own, b_both, tree_s, a0_r, peer)
    for level in range(6, 1, -1):
        @pl.when(flag(level))
        def _(level=level):
            send(lg_own.at[level, other], lg_both.at[level], level_s.at[level - 1], b0_r.at[level - 1], peer)

    @pl.when(core == 1)
    def _():
        send(lg_own.at[1], state, level_s.at[0], b0_r.at[0], peer)

    scale_level(0)

    arrived(b_both, a0_r)
    lg_sum[0] = (b_own[core].astype(F32) + b_both[core].astype(F32)).astype(BF16)
    for step in z_order:
        zt = z_at(step)
        send(lg_sum.at[0, zt], a_slabs.at[z], tree_s, a1_r, at(x, zt, core))
    a_slabs[z] = lg_sum[0, z]

    for level in (6, 5, 4, 3, 2):
        @pl.when(flag(level))
        def _(level=level):
            arrived(lg_both.at[level], b0_r.at[level - 1])
            lg_sum[level] = (lg_own[level, core].astype(F32) + lg_both[level].astype(F32)).astype(BF16)
            for step in z_order:
                zt = z_at(step)
                send(
                    lg_sum.at[level, zt], b_slabs.at[level, z], level_s.at[level - 1],
                    b1_r.at[level - 2], at(x, zt, core),
                )
            b_slabs[level, z] = lg_sum[level, z]

    def block_tile(j):
        rows = slice(j * TILE, (j + 1) * TILE)
        later = slice(j * TILE, tokens)
        count = tokens - j * TILE
        keep = lax.broadcasted_iota(jnp.int32, (TILE, count), 1) >= lax.broadcasted_iota(
            jnp.int32, (TILE, count), 0
        )
        masked_t = jnp.where(keep, rows_by_rows(k_ref[rows, :], q_ref[later, :]), 0.0).astype(BF16)
        v_acc[rows, :] = plain(masked_t, scaled[0, later, :])
        grad_t = jnp.where(keep, rows_by_rows(v_ref[rows, :], scaled[0, later, :]), 0.0).astype(BF16)
        k_acc[rows, :] = plain(grad_t, q_ref[later, :])
        term = cols_by_cols(grad_t, k_ref[rows, :])
        if j == 0:
            q_acc[...] = term
        else:
            q_acc[later, :] += term

    block_tile(0)

    arrived(a_slabs.at[pl.ds(0, NZ - 1)], a1_r)
    tier1 = [a_slabs[i].astype(F32) for i in range(NZ)]
    tier2 = [(tier1[2 * i] + tier1[2 * i + 1]).astype(BF16) for i in range(4)]
    tier3 = [(tier2[2 * i].astype(F32) + tier2[2 * i + 1].astype(F32)).astype(BF16) for i in range(2)]
    tier4 = (tier3[0].astype(F32) + tier3[1].astype(F32)).astype(BF16)
    for i in range(4):
        t2_buf[i] = tier2[i]
    t3_buf[...] = tier3[0]
    t4_slots[x] = tier4
    for step in range(1, NX):
        send(t4_slots.at[x], t4_slots.at[x], tree_s, a2_r, at(x_at(step), z, core))

    def sib_src(level, zt):
        if level == 2:
            return a_slabs.at[zt - 1]
        if level == 3:
            return t2_buf.at[lax.div(zt, 2) - 1]
        if level == 4:
            return t3_buf
        if level == 5:
            return t4_slots.at[x - 1]
        return t5_buf

    def reads(level, zt):
        if level >= 5:
            return flag(level)
        return lax.rem(lax.div(zt, 2 ** (level - 2)), 2) == 1

    def send_sibling(level, step):
        zt = z_at(step)
        send(
            sib_src(level, zt), sib.at[level, core, z], level_s.at[level - 1],
            a3_r.at[level - 2], at(x, zt, core),
        )

    def keep_sibling(level):
        sib[level, core, z] = sib_src(level, z)[...]

    for step in z_order:
        for level in (4, 3, 2):
            @pl.when(reads(level, z_at(step)))
            def _(level=level, step=step):
                send_sibling(level, step)
    for level in (4, 3, 2):
        @pl.when(flag(level))
        def _(level=level):
            keep_sibling(level)

    block_tile(1)


    def slab_sum(level):
        arrived(b_slabs.at[level, pl.ds(0, NZ - 1)], b1_r.at[level - 2])
        total = b_slabs[level, 0].astype(F32)
        for i in range(1, NZ):
            total += b_slabs[level, i].astype(F32)
        return total.astype(BF16)

    @pl.when(flag(6))
    def _():
        s_own[1] = slab_sum(6)
        send(s_own.at[1], s_slots.at[x - 1], level_s.at[5], b2_r.at[1], at(0, z, core))
        send(s_own.at[1], s_slots.at[x - 1], level_s.at[5], b2_r.at[1], at(1, z, core))

    @pl.when(flag(5))
    def _():
        s_own[0] = slab_sum(5)
        send(s_own.at[0], s_slots.at[0], level_s.at[4], b2_r.at[0], at(x - 1, z, core))

    arrived(t4_slots.at[pl.ds(0, NX - 1)], a2_r)
    t5_buf[...] = (t4_slots[0].astype(F32) + t4_slots[1].astype(F32)).astype(BF16)
    for level in (6, 5):
        @pl.when(flag(level))
        def _(level=level):
            for step in z_order:
                send_sibling(level, step)
            keep_sibling(level)

    block_tile(2)
    block_tile(3)

    for level in (2, 3, 4):
        @pl.when(flag(level))
        def _(level=level):
            arrived(b_slabs.at[level, pl.ds(0, 3)], b1_r.at[level - 2])

        @pl.when(jnp.logical_not(flag(level)))
        def _(level=level):
            arrived(b_slabs.at[level, pl.ds(0, 4)], b1_r.at[level - 2])


    @pl.when(lax.rem(x, 2) == 0)
    def _():
        arrived(s_slots.at[0], b2_r.at[0])

    @pl.when(lax.div(x, 2) == 0)
    def _():
        arrived(s_slots.at[pl.ds(1, 2)], b2_r.at[1])

    zero = jnp.zeros((SLAB, HALF), F32)
    far = jnp.where(lax.rem(x, 2) == 0, s_slots[0].astype(F32), zero)
    far += jnp.where(lax.div(x, 2) == 0, s_slots[1].astype(F32) + s_slots[2].astype(F32), zero)
    upper = b_slabs[4, 4].astype(F32)
    for i in (5, 6, 7):
        upper += b_slabs[4, i].astype(F32)
    for zt in range(NZ):
        total = far
        if zt < 4:
            total = total + upper
        if zt % 4 < 2:
            base = zt - zt % 4
            total = total + b_slabs[3, base + 2].astype(F32) + b_slabs[3, base + 3].astype(F32)
        if zt % 2 == 0:
            total = total + b_slabs[2, zt + 1].astype(F32)
        s_own[2 + zt] = total.astype(BF16)
    for step in z_order:
        zt = z_at(step)
        send(s_own.at[2 + zt], g_buf.at[core, z], tree_s, b3_r, at(x, zt, core))
    g_buf[core, z] = s_own[2 + z]

    for level in (2, 3, 4, 5, 6):
        @pl.when(flag(level))
        def _(level=level):
            arrived(sib.at[level, core, pl.ds(0, NZ - 1)], a3_r.at[level - 2])
            send(sib.at[level, core], sib.at[level, core], level_s.at[level - 1], a4_r.at[level - 2], peer)


    def add_sibling(level, halves):
        for half in range(2):
            block = halves(half).reshape(NZ * SLAB, HALF)
            q_acc[...] += rows_by_rows(scaled[level, :, half * HALF:(half + 1) * HALF], block)

    @pl.when(core == 1)
    def _():
        add_sibling(1, lambda half: b_both[half])

    for level in (2, 3, 4, 5, 6):
        @pl.when(flag(level))
        def _(level=level):
            arrived(sib.at[level, other], a4_r.at[level - 2])
            add_sibling(level, lambda half: sib[level, half])

    def start_sum(acc, part, relay, slots, r_sem):
        part[...] = acc[...].astype(BF16).reshape(part.shape)
        send(part.at[y_at(-4)], relay.at[1], head_s, r_sem.at[0], (seq, y_at(-2)))
        send(part.at[y_at(-3)], relay.at[0], head_s, r_sem.at[0], (seq, y_at(-1)))
        send(part.at[y_at(3)], relay.at[2], head_s, r_sem.at[1], (seq, y_at(1)))
        send(part.at[y_at(-1)], slots.at[0], head_s, r_sem.at[2], (seq, y_at(-1)))
        send(part.at[y_at(1)], slots.at[1], head_s, r_sem.at[2], (seq, y_at(1)))

    def relay_sum(part, relay, slots, r_sem):
        arrived(relay.at[pl.ds(0, 2)], r_sem.at[0])
        relay[3] = (
            part[y_at(-2)].astype(F32) + relay[0].astype(F32) + relay[1].astype(F32)
        ).astype(BF16)
        send(relay.at[3], slots.at[2], head_s, r_sem.at[2], (seq, y_at(-2)))
        arrived(relay.at[2], r_sem.at[1])
        relay[4] = (part[y_at(2)].astype(F32) + relay[2].astype(F32)).astype(BF16)
        send(relay.at[4], slots.at[3], head_s, r_sem.at[2], (seq, y_at(2)))

    def finish_sum(part, slots, out, r_sem):
        arrived(slots, r_sem.at[2])
        total = part[y].astype(F32)
        for i in range(4):
            total += slots[i].astype(F32)
        out[y] = total.astype(BF16)
        send(out.at[y], out.at[y], head_s, r_sem.at[3], (seq, y_at(2)))
        send(out.at[y], out.at[y], head_s, r_sem.at[4], (seq, y_at(-2)))
        send(out.at[y], out.at[y], head_s, r_sem.at[5], (seq, y_at(1)))
        send(out.at[y], out.at[y], head_s, r_sem.at[5], (seq, y_at(-1)))

    def hand_on(out, r_sem):
        below, above = y_at(-2), y_at(2)
        arrived(out.at[below], r_sem.at[3])
        send(out.at[below], out.at[below], head_s, r_sem.at[5], (seq, y_at(2)))
        send(out.at[below], out.at[below], head_s, r_sem.at[5], (seq, y_at(1)))
        arrived(out.at[above], r_sem.at[4])
        send(out.at[above], out.at[above], head_s, r_sem.at[5], (seq, y_at(-1)))

    start_sum(q_acc, q_part, q_relay, q_slots, q_r)

    arrived(g_buf.at[core, pl.ds(0, NZ - 1)], b3_r)
    send(g_buf.at[core], g_buf.at[core], tree_s, b4_r, peer)

    @pl.when(core == 0)
    def _():
        arrived(state, b0_r.at[0])

    arrived(g_buf.at[other], b4_r)
    near = jnp.where(core == 0, state[...].astype(F32), 0.0)
    low = (near + g_buf[...].astype(F32)).astype(BF16).reshape(2, NZ * SLAB, HALF)
    for half in range(2):
        k_acc[...] += rows_by_rows(v_ref[:, half * HALF:(half + 1) * HALF], low[half])
    start_sum(k_acc, k_part, k_relay, k_slots, k_r)
    relay_sum(q_part, q_relay, q_slots, q_r)

    for half in range(2):
        cols = slice(half * HALF, (half + 1) * HALF)
        vg_ref[:, cols] = (v_acc[:, cols] + plain(k_ref[...], low[half])).astype(BF16)

    relay_sum(k_part, k_relay, k_slots, k_r)
    finish_sum(q_part, q_slots, qg_ref, q_r)
    finish_sum(k_part, k_slots, kg_ref, k_r)
    hand_on(qg_ref, q_r)
    hand_on(kg_ref, k_r)

    sent(328, tree_s)

    @pl.when(core == 1)
    def _():
        sent(128, level_s.at[0])

    for level, bytes_set, bytes_unset in ((2, 208, 32), (3, 208, 32), (4, 208, 32), (5, 248, 0), (6, 256, 0)):
        @pl.when(flag(level))
        def _(level=level, bytes_set=bytes_set):
            sent(bytes_set, level_s.at[level - 1])

        if bytes_unset:
            @pl.when(jnp.logical_not(flag(level)))
            def _(level=level, bytes_unset=bytes_unset):
                sent(bytes_unset, level_s.at[level - 1])

    arrived(qg_ref.at[pl.ds(0, 5)], q_r.at[5])
    arrived(kg_ref.at[pl.ds(0, 5)], k_r.at[5])
    sent(896, head_s)


def write_out(q_in, k_in, v_in, q_out, k_out, v_out, sems):
    copies = [
        pltpu.make_async_copy(src, dst, sems.at[i])
        for i, (src, dst) in enumerate(((v_in, v_out), (q_in, q_out), (k_in, k_out)))
    ]
    for copy in copies:
        copy.start()
    for copy in copies:
        copy.wait()


def per_device(queries, key_rows, value_rows, out_grad, level_index, level_table):
    tokens, state_size = queries.shape
    columns = value_rows.shape[1]
    anywhere = pl.BlockSpec(memory_space=pl.ANY)
    held = pl.BlockSpec(memory_space=pltpu.VMEM)
    dma = pltpu.SemaphoreType.DMA
    half = (NZ, SLAB, HALF)
    slots = (NY, tokens // NY, state_size)
    part = slots[1:]
    ladder = LEVELS - 1
    scratch = [
        pltpu.VMEM(queries.shape, BF16),
        pltpu.VMEM(key_rows.shape, BF16),
        pltpu.VMEM(value_rows.shape, BF16),
        pltpu.VMEM(out_grad.shape, BF16),
        pltpu.VMEM((LEVELS, tokens), jnp.int32),
        pltpu.VMEM(level_table.shape, F32),
        pltpu.VMEM((LEVELS, tokens, columns), BF16),
        pltpu.VMEM((LEVELS, 2 * PICKS, columns), BF16),
        pltpu.VMEM((state_size, tokens), BF16),
        pltpu.VMEM((tokens, state_size), F32),
        pltpu.VMEM((tokens, state_size), F32),
        pltpu.VMEM((tokens, columns), F32),
        pltpu.VMEM((2,) + half, BF16),
        pltpu.VMEM((2,) + half, BF16),
        pltpu.VMEM(half, BF16),
        pltpu.VMEM((4, SLAB, HALF), BF16),
        pltpu.VMEM((SLAB, HALF), BF16),
        pltpu.VMEM((NX, SLAB, HALF), BF16),
        pltpu.VMEM((SLAB, HALF), BF16),
        pltpu.VMEM((LEVELS, 2) + half, BF16),
        pltpu.VMEM((LEVELS, 2) + half, BF16),
        pltpu.VMEM((LEVELS,) + half, BF16),
        pltpu.VMEM((LEVELS,) + half, BF16),
        pltpu.VMEM((LEVELS,) + half, BF16),
        pltpu.VMEM((2 + NZ, SLAB, HALF), BF16),
        pltpu.VMEM((3, SLAB, HALF), BF16),
        pltpu.VMEM((2,) + half, BF16),
        pltpu.VMEM((2,) + half, BF16),
        pltpu.VMEM(slots, BF16),
        pltpu.VMEM(slots, BF16),
        pltpu.VMEM((5,) + part, BF16),
        pltpu.VMEM((5,) + part, BF16),
        pltpu.VMEM((4,) + part, BF16),
        pltpu.VMEM((4,) + part, BF16),
        dma((6,)), dma, dma, dma((ladder,)),
        dma, dma, dma, dma((ladder - 1,)), dma((ladder - 1,)), dma((ladder,)), dma((ladder - 1,)),
        dma((2,)), dma, dma, dma((6,)), dma((6,)),
    ]
    query_grad, key_grad, value_grad = pl.pallas_call(
        kernel,
        out_shape=(
            pltpu.VMEM(slots, BF16),
            pltpu.VMEM(slots, BF16),
            pltpu.VMEM((tokens, columns), BF16),
        ),
        in_specs=[anywhere] * 6,
        out_specs=(held, held, held),
        scratch_shapes=scratch,
        compiler_params=pltpu.CompilerParams(
            collective_id=0, has_side_effects=True, vmem_limit_bytes=40 * 1024 * 1024
        ),
        name="fenwick_backward",
    )(
        *(
            pltpu.with_memory_space_constraint(operand, pltpu.HBM)
            for operand in (queries, key_rows, value_rows, out_grad, level_index.T, level_table)
        )
    )
    query_grad, key_grad, value_grad = pl.pallas_call(
        write_out,
        out_shape=(
            jax.ShapeDtypeStruct(slots, BF16),
            jax.ShapeDtypeStruct(slots, BF16),
            jax.ShapeDtypeStruct((tokens, columns), BF16),
        ),
        in_specs=[held] * 3,
        out_specs=(anywhere, anywhere, anywhere),
        scratch_shapes=[dma((3,))],
        name="write_out",
    )(*(pltpu.with_memory_space_constraint(g, pltpu.VMEM) for g in (query_grad, key_grad, value_grad)))
    return (
        query_grad.reshape(tokens, state_size),
        key_grad.reshape(tokens, state_size),
        value_grad,
    )


def solution(mesh):
    return jax.shard_map(
        per_device,
        mesh=mesh,
        in_specs=(
            P("seq", None),
            P("seq", None),
            P("seq", "head"),
            P("seq", "head"),
            P("seq", None),
            P(None, None, "head"),
        ),
        out_specs=(P("seq", None), P("seq", None), P("seq", "head")),
        check_vma=False,
    )
```

time: 221 us -> 55.3 us (0.25)
  waiting for transfers between devices: 129 us -> 0 us
  Pallas kernels: 0 us -> 54.5 us
  starting transfers between devices: 47.4 us -> 0 us
  matrix products: 18.3 us -> 0 us
  between operations: 14.5 us -> 0.64 us
  local copies, waits for them, and re-layouts: 5.83 us -> 0 us
  other arithmetic: 5.31 us -> 0 us
    psum x1 -> x0, waiting for transfers between devices: 73 us -> none  [per_device(): lax.psum(query_grad.astype(jnp.bfloat16), 'head').astype(jnp.float32)]
    ppermute x12 -> x0, waiting for transfers between devices: 55.6 us -> none  [swapped(): return lax.ppermute(block, axis, route)]
    pallas_call x0 -> x2, Pallas kernels: none -> 54.5 us  [the longest x1 53.3 us: per_device(): pl.pallas_call(kernel, out_shape=(pltpu.VMEM(slots, BF16), pltpu.VMEM(slo...]
    ppermute x12 -> x0, starting transfers between devices: 47.3 us -> none  [swapped(): return lax.ppermute(block, axis, route)]
    dot_general x19 -> x0, matrix products: 18.3 us -> none  [the longest x9 8.47 us: contract_rows(): lax.dot_general(left, right, (((0,), (0,)), ((), ())), preferred_element_...]
    unnamed x19 -> x0, local copies, waits for them, and re-layouts: 5.12 us -> none
    convert_element_type x17 -> x0, other arithmetic: 4.95 us -> none  [the longest x1 2.79 us: scale_by(): (shaped * weights[:, height, :, None]).reshape(rows_here, columns)]
  transfers between devices with their start and end apart: 13 -> 0, of which waited for: 7 -> 0; matrix products, arithmetic and copies ran while one was open for 10% -> 0% of each run, Pallas kernels for 0% -> 0%
where the time goes in v2:
time: 55.3 us; the launch traced here: 55.1 us
  Pallas kernels  54.5 us (99%)
  between operations  0.64 us (1%)
    pallas_call x1, Pallas kernels, per_device(): pl.pallas_call(kernel, out_shape=(pltpu.VMEM(slots, BF16), pltpu.VMEM(slo...  53.3 us
    pallas_call x1, Pallas kernels, per_device(): pl.pallas_call(write_out, out_shape=(jax.ShapeDtypeStruct(slots, BF16), j...  1.16 us

profile of v2, /device:TPU:6, one launch (start us, length us, event | category | flops | bytes accessed | tf_op | source)
XLA Modules:
  0.0 55.1 jit_solution(3712437383958180114)
XLA Ops:
  0.6 53.3 %fenwick_backward.1 = (bf16[8,128,128]{2,1,0:T(8,128)(2,1)S(1)}, bf16[8,128,128]{2,1,0:T(8,128)(2,1)S(1)}, bf16[1024,512]{1,0:T(8,128)(2,1)S(1)}) custom-call(bf16[1024,128]{1,0:T(8,128)(2,1)} %q_in.1, bf16[1024,128]{1,0:T(8,128)(2,1)} %k_in.1, bf16[1024,512]{1,0:T(8,128)(2,1)} %v_in.1, bf16[1024,512]{1,0:T(8,128)(2,1)} %og_in.1, s32[7,1024]{1,0:T(8,128)} %bitcast.3, ...), custom_call_target="tpu_custom_call" | custom-call | tf_op jit(solution)/shard_map/fenwick_backward/pallas_call | solution.py:485
  54.0 1.2 %write_out.1 = (bf16[8,128,128]{2,1,0:T(8,128)(2,1)}, bf16[8,128,128]{2,1,0:T(8,128)(2,1)}, bf16[1024,512]{1,0:T(8,128)(2,1)}) custom-call(bf16[8,128,128]{2,1,0:T(8,128)(2,1)S(1)} %get-tuple-element.9.q_in, bf16[8,128,128]{2,1,0:T(8,128)(2,1)S(1)} %get-tuple-element.10.k_in, bf16[1024,512]{1,0:T(8,128)(2,1)S(1)} %get-tuple-element.11.v_in), custom_call_target="tpu_custom_call" | custom-call | tf_op jit(solution)/shard_map/write_out/pallas_call | solution.py:505

commit v3 on v2

--- a/solution.py
+++ b/solution.py
@@ -15,6 +15,8 @@
 SLAB = 16
 HALF = 256
 TILE = 256
+EARLY = (6, 5, 4)
+LATE = (3, 2, 1)
 
 
 def rows_by_rows(left, right):
@@ -34,11 +36,11 @@
     qg_ref, kg_ref, vg_ref,
     q_ref, k_ref, v_ref, og_ref, idx_ref, table_ref,
     scaled, picks, q_turned, q_acc, k_acc, v_acc,
-    b_own, b_both, a_slabs, t2_buf, t3_buf, t4_slots, t5_buf, sib,
-    lg_own, lg_both, lg_sum, b_slabs, s_own, s_slots, g_buf, state,
+    b_own, b_both, a_slabs, t2_buf, t3_buf, t4_buf, far_sib, sib,
+    lg_own, lg_both, lg_sum, b_slabs, five_slabs, six_slabs, g_own, g_buf, state,
     q_part, k_part, q_relay, k_relay, q_slots, k_slots,
     in_sem, tree_s, head_s, level_s,
-    a0_r, a1_r, a2_r, a3_r, a4_r, b0_r, b1_r, b2_r, b3_r, b4_r, q_r, k_r,
+    a0_r, a1_r, a3_r, a4_r, b0_r, b1_r, b3_r, b4_r, q_r, k_r,
 ):
     seq = lax.axis_index("seq")
     y = lax.axis_index("head")
@@ -84,16 +86,7 @@
             device_id=peer, device_id_type=MESH,
         ).wait_send()
 
-    z_order = [1, 7, 2, 6, 3, 5, 4]
-
-    barrier = pltpu.get_barrier_semaphore()
-    for step in range(1, NZ):
-        pl.semaphore_signal(barrier, inc=1, device_id=at(x, z_at(step), core), device_id_type=MESH)
-    for step in range(1, NX):
-        pl.semaphore_signal(barrier, inc=1, device_id=at(x_at(step), z, core), device_id_type=MESH)
-    for step in (2, -2, 1, -1):
-        pl.semaphore_signal(barrier, inc=1, device_id=(seq, y_at(step)), device_id_type=MESH)
-    pl.semaphore_signal(barrier, inc=1, device_id=peer, device_id_type=MESH)
+    z_order = [4, 3, 5, 2, 6, 1, 7]
 
     loads = [
         pltpu.make_async_copy(src, dst, in_sem.at[i])
@@ -102,7 +95,20 @@
             (idx_in, idx_ref), (og_in, og_ref), (q_in, q_ref),
         ))
     ]
-    for load in loads:
+    loads[0].start()
+    loads[1].start()
+
+    barrier = pltpu.get_barrier_semaphore()
+    for x_step in (2, 3, 1, 0):
+        for step in z_order if x_step == 0 else z_order + [0]:
+            pl.semaphore_signal(
+                barrier, inc=1, device_id=at(x_at(x_step), z_at(step), core), device_id_type=MESH
+            )
+    for step in (2, -2, 1, -1):
+        pl.semaphore_signal(barrier, inc=1, device_id=(seq, y_at(step)), device_id_type=MESH)
+    pl.semaphore_signal(barrier, inc=1, device_id=peer, device_id_type=MESH)
+
+    for load in loads[2:]:
         load.start()
 
     loads[0].wait()
@@ -136,25 +142,48 @@
     def flag(level):
         return lax.rem(lax.div(seq, 2 ** (level - 1)), 2) == 1
 
-    for level in range(6, 0, -1):
+    def level_grad(level):
         scale_level(level)
         product = plain(q_turned[...], scaled[level]).astype(BF16)
         for half in range(2):
             lg_own[level, half] = product[:, half * HALF:(half + 1) * HALF].reshape(NZ, SLAB, HALF)
 
-    pl.semaphore_wait(barrier, 1 + (NZ - 1) + (NX - 1) + 4)
-
+    def swap_level(level):
+        @pl.when(flag(level))
+        def _():
+            send(
+                lg_own.at[level, other], lg_both.at[level], level_s.at[level - 1],
+                b0_r.at[level - 1], peer,
+            )
+
+    def hand_level(level):
+        @pl.when(flag(level))
+        def _():
+            arrived(lg_both.at[level], b0_r.at[level - 1])
+            lg_sum[level] = (lg_own[level, core].astype(F32) + lg_both[level].astype(F32)).astype(BF16)
+            for step in z_order if level < 5 else z_order + [0]:
+                zt = z_at(step)
+                part = lg_sum.at[level, zt]
+                if level == 6:
+                    targets = ((six_slabs.at[x - 2, z], at(0, zt, core)), (six_slabs.at[x - 2, z], at(1, zt, core)))
+                elif level == 5:
+                    targets = ((five_slabs.at[z], at(x - 1, zt, core)),)
+                else:
+                    targets = ((b_slabs.at[level, z], at(x, zt, core)),)
+                for slot, to in targets:
+                    send(part, slot, level_s.at[level - 1], b1_r.at[level - 2], to)
+            if level < 5:
+                b_slabs[level, z] = lg_sum[level, z]
+
+    for level in EARLY:
+        level_grad(level)
+
+    pl.semaphore_wait(barrier, 1 + (NX * NZ - 1) + 4)
     send(b_own, b_both, tree_s, a0_r, peer)
-    for level in range(6, 1, -1):
-        @pl.when(flag(level))
-        def _(level=level):
-            send(lg_own.at[level, other], lg_both.at[level], level_s.at[level - 1], b0_r.at[level - 1], peer)
-
-    @pl.when(core == 1)
-    def _():
-        send(lg_own.at[1], state, level_s.at[0], b0_r.at[0], peer)
-
-    scale_level(0)
+    for level in EARLY:
+        swap_level(level)
+    level_grad(LATE[0])
+    swap_level(LATE[0])
 
     arrived(b_both, a0_r)
     lg_sum[0] = (b_own[core].astype(F32) + b_both[core].astype(F32)).astype(BF16)
@@ -163,18 +192,19 @@
         send(lg_sum.at[0, zt], a_slabs.at[z], tree_s, a1_r, at(x, zt, core))
     a_slabs[z] = lg_sum[0, z]
 
-    for level in (6, 5, 4, 3, 2):
-        @pl.when(flag(level))
-        def _(level=level):
-            arrived(lg_both.at[level], b0_r.at[level - 1])
-            lg_sum[level] = (lg_own[level, core].astype(F32) + lg_both[level].astype(F32)).astype(BF16)
-            for step in z_order:
-                zt = z_at(step)
-                send(
-                    lg_sum.at[level, zt], b_slabs.at[level, z], level_s.at[level - 1],
-                    b1_r.at[level - 2], at(x, zt, core),
-                )
-            b_slabs[level, z] = lg_sum[level, z]
+    for level in EARLY:
+        hand_level(level)
+    for before, level in zip(LATE, LATE[1:]):
+        level_grad(level)
+        if level > 1:
+            swap_level(level)
+        hand_level(before)
+
+    @pl.when(core == 1)
+    def _():
+        send(lg_own.at[1], state, level_s.at[0], b0_r.at[0], peer)
+
+    scale_level(0)
 
     def block_tile(j):
         rows = slice(j * TILE, (j + 1) * TILE)
@@ -203,24 +233,16 @@
     for i in range(4):
         t2_buf[i] = tier2[i]
     t3_buf[...] = tier3[0]
-    t4_slots[x] = tier4
-    for step in range(1, NX):
-        send(t4_slots.at[x], t4_slots.at[x], tree_s, a2_r, at(x_at(step), z, core))
+    t4_buf[...] = tier4
 
     def sib_src(level, zt):
         if level == 2:
             return a_slabs.at[zt - 1]
         if level == 3:
             return t2_buf.at[lax.div(zt, 2) - 1]
-        if level == 4:
-            return t3_buf
-        if level == 5:
-            return t4_slots.at[x - 1]
-        return t5_buf
+        return t3_buf
 
     def reads(level, zt):
-        if level >= 5:
-            return flag(level)
         return lax.rem(lax.div(zt, 2 ** (level - 2)), 2) == 1
 
     def send_sibling(level, step):
@@ -233,6 +255,18 @@
     def keep_sibling(level):
         sib[level, core, z] = sib_src(level, z)[...]
 
+    for step in z_order + [0]:
+        zt = z_at(step)
+
+        @pl.when(lax.div(x, 2) == 0)
+        def _(zt=zt):
+            for x_to in (2, 3):
+                send(t4_buf, far_sib.at[x, z], level_s.at[5], a3_r.at[4], at(x_to, zt, core))
+
+        @pl.when(lax.rem(x, 2) == 0)
+        def _(zt=zt):
+            send(t4_buf, sib.at[5, core, z], level_s.at[4], a3_r.at[3], at(x + 1, zt, core))
+
     for step in z_order:
         for level in (4, 3, 2):
             @pl.when(reads(level, z_at(step)))
@@ -243,35 +277,18 @@
         def _(level=level):
             keep_sibling(level)
 
+    def half_of(which):
+        return pl.ds(pl.multiple_of(which * HALF, HALF), HALF)
+
+    def add_sibling(level, which, slabs):
+        q_acc[...] += rows_by_rows(scaled[level, :, half_of(which)], slabs.reshape(NZ * SLAB, HALF))
+
+    @pl.when(core == 1)
+    def _():
+        for half in range(2):
+            add_sibling(1, half, b_both[half])
+
     block_tile(1)
-
-
-    def slab_sum(level):
-        arrived(b_slabs.at[level, pl.ds(0, NZ - 1)], b1_r.at[level - 2])
-        total = b_slabs[level, 0].astype(F32)
-        for i in range(1, NZ):
-            total += b_slabs[level, i].astype(F32)
-        return total.astype(BF16)
-
-    @pl.when(flag(6))
-    def _():
-        s_own[1] = slab_sum(6)
-        send(s_own.at[1], s_slots.at[x - 1], level_s.at[5], b2_r.at[1], at(0, z, core))
-        send(s_own.at[1], s_slots.at[x - 1], level_s.at[5], b2_r.at[1], at(1, z, core))
-
-    @pl.when(flag(5))
-    def _():
-        s_own[0] = slab_sum(5)
-        send(s_own.at[0], s_slots.at[0], level_s.at[4], b2_r.at[0], at(x - 1, z, core))
-
-    arrived(t4_slots.at[pl.ds(0, NX - 1)], a2_r)
-    t5_buf[...] = (t4_slots[0].astype(F32) + t4_slots[1].astype(F32)).astype(BF16)
-    for level in (6, 5):
-        @pl.when(flag(level))
-        def _(level=level):
-            for step in z_order:
-                send_sibling(level, step)
-            keep_sibling(level)
 
     block_tile(2)
     block_tile(3)
@@ -285,18 +302,21 @@
         def _(level=level):
             arrived(b_slabs.at[level, pl.ds(0, 4)], b1_r.at[level - 2])
 
-
     @pl.when(lax.rem(x, 2) == 0)
     def _():
-        arrived(s_slots.at[0], b2_r.at[0])
+        arrived(five_slabs, b1_r.at[3])
 
     @pl.when(lax.div(x, 2) == 0)
     def _():
-        arrived(s_slots.at[pl.ds(1, 2)], b2_r.at[1])
-
+        arrived(six_slabs, b1_r.at[4])
+
+    five = five_slabs[0].astype(F32)
+    six = six_slabs[0, 0].astype(F32) + six_slabs[1, 0].astype(F32)
+    for i in range(1, NZ):
+        five += five_slabs[i].astype(F32)
+        six += six_slabs[0, i].astype(F32) + six_slabs[1, i].astype(F32)
     zero = jnp.zeros((SLAB, HALF), F32)
-    far = jnp.where(lax.rem(x, 2) == 0, s_slots[0].astype(F32), zero)
-    far += jnp.where(lax.div(x, 2) == 0, s_slots[1].astype(F32) + s_slots[2].astype(F32), zero)
+    far = jnp.where(lax.rem(x, 2) == 0, five, zero) + jnp.where(lax.div(x, 2) == 0, six, zero)
     upper = b_slabs[4, 4].astype(F32)
     for i in (5, 6, 7):
         upper += b_slabs[4, i].astype(F32)
@@ -309,33 +329,11 @@
             total = total + b_slabs[3, base + 2].astype(F32) + b_slabs[3, base + 3].astype(F32)
         if zt % 2 == 0:
             total = total + b_slabs[2, zt + 1].astype(F32)
-        s_own[2 + zt] = total.astype(BF16)
+        g_own[zt] = total.astype(BF16)
     for step in z_order:
         zt = z_at(step)
-        send(s_own.at[2 + zt], g_buf.at[core, z], tree_s, b3_r, at(x, zt, core))
-    g_buf[core, z] = s_own[2 + z]
-
-    for level in (2, 3, 4, 5, 6):
-        @pl.when(flag(level))
-        def _(level=level):
-            arrived(sib.at[level, core, pl.ds(0, NZ - 1)], a3_r.at[level - 2])
-            send(sib.at[level, core], sib.at[level, core], level_s.at[level - 1], a4_r.at[level - 2], peer)
-
-
-    def add_sibling(level, halves):
-        for half in range(2):
-            block = halves(half).reshape(NZ * SLAB, HALF)
-            q_acc[...] += rows_by_rows(scaled[level, :, half * HALF:(half + 1) * HALF], block)
-
-    @pl.when(core == 1)
-    def _():
-        add_sibling(1, lambda half: b_both[half])
-
-    for level in (2, 3, 4, 5, 6):
-        @pl.when(flag(level))
-        def _(level=level):
-            arrived(sib.at[level, other], a4_r.at[level - 2])
-            add_sibling(level, lambda half: sib[level, half])
+        send(g_own.at[zt], g_buf.at[core, z], tree_s, b3_r, at(x, zt, core))
+    g_buf[core, z] = g_own[z]
 
     def start_sum(acc, part, relay, slots, r_sem):
         part[...] = acc[...].astype(BF16).reshape(part.shape)
@@ -374,6 +372,27 @@
         arrived(out.at[above], r_sem.at[4])
         send(out.at[above], out.at[above], head_s, r_sem.at[5], (seq, y_at(-1)))
 
+    for level in (6, 5, 4, 3, 2):
+        @pl.when(flag(level))
+        def _(level=level):
+            if level == 6:
+                arrived(far_sib, a3_r.at[4])
+                sib[6, core] = (far_sib[0].astype(F32) + far_sib[1].astype(F32)).astype(BF16)
+            else:
+                arrived(sib.at[level, core, pl.ds(0, NZ - 1 if level < 5 else NZ)], a3_r.at[level - 2])
+            send(sib.at[level, core], sib.at[level, core], level_s.at[level - 1], a4_r.at[level - 2], peer)
+
+    for level in (6, 5, 4, 3, 2):
+        @pl.when(flag(level))
+        def _(level=level):
+            add_sibling(level, core, sib[level, core])
+
+    for level in (6, 5, 4, 3, 2):
+        @pl.when(flag(level))
+        def _(level=level):
+            arrived(sib.at[level, other], a4_r.at[level - 2])
+            add_sibling(level, other, sib[level, other])
+
     start_sum(q_acc, q_part, q_relay, q_slots, q_r)
 
     arrived(g_buf.at[core, pl.ds(0, NZ - 1)], b3_r)
@@ -383,17 +402,20 @@
     def _():
         arrived(state, b0_r.at[0])
 
+    def state_low(half):
+        near = jnp.where(core == 0, state[half].astype(F32), 0.0)
+        return (near + g_buf[half].astype(F32)).astype(BF16).reshape(NZ * SLAB, HALF)
+
+    k_acc[...] += rows_by_rows(v_ref[:, half_of(core)], state_low(core))
     arrived(g_buf.at[other], b4_r)
-    near = jnp.where(core == 0, state[...].astype(F32), 0.0)
-    low = (near + g_buf[...].astype(F32)).astype(BF16).reshape(2, NZ * SLAB, HALF)
-    for half in range(2):
-        k_acc[...] += rows_by_rows(v_ref[:, half * HALF:(half + 1) * HALF], low[half])
+    k_acc[...] += rows_by_rows(v_ref[:, half_of(other)], state_low(other))
     start_sum(k_acc, k_part, k_relay, k_slots, k_r)
+
     relay_sum(q_part, q_relay, q_slots, q_r)
 
     for half in range(2):
         cols = slice(half * HALF, (half + 1) * HALF)
-        vg_ref[:, cols] = (v_acc[:, cols] + plain(k_ref[...], low[half])).astype(BF16)
+        vg_ref[:, cols] = (v_acc[:, cols] + plain(k_ref[...], state_low(half))).astype(BF16)
 
     relay_sum(k_part, k_relay, k_slots, k_r)
     finish_sum(q_part, q_slots, qg_ref, q_r)
@@ -401,13 +423,13 @@
     hand_on(qg_ref, q_r)
     hand_on(kg_ref, k_r)
 
-    sent(328, tree_s)
+    sent(304, tree_s)
 
     @pl.when(core == 1)
     def _():
         sent(128, level_s.at[0])
 
-    for level, bytes_set, bytes_unset in ((2, 208, 32), (3, 208, 32), (4, 208, 32), (5, 248, 0), (6, 256, 0)):
+    for level, bytes_set, bytes_unset in ((2, 208, 32), (3, 208, 32), (4, 208, 32), (5, 192, 64), (6, 256, 128)):
         @pl.when(flag(level))
         def _(level=level, bytes_set=bytes_set):
             sent(bytes_set, level_s.at[level - 1])
@@ -461,15 +483,16 @@
         pltpu.VMEM(half, BF16),
         pltpu.VMEM((4, SLAB, HALF), BF16),
         pltpu.VMEM((SLAB, HALF), BF16),
-        pltpu.VMEM((NX, SLAB, HALF), BF16),
         pltpu.VMEM((SLAB, HALF), BF16),
+        pltpu.VMEM((2,) + half, BF16),
         pltpu.VMEM((LEVELS, 2) + half, BF16),
         pltpu.VMEM((LEVELS, 2) + half, BF16),
         pltpu.VMEM((LEVELS,) + half, BF16),
         pltpu.VMEM((LEVELS,) + half, BF16),
         pltpu.VMEM((LEVELS,) + half, BF16),
-        pltpu.VMEM((2 + NZ, SLAB, HALF), BF16),
-        pltpu.VMEM((3, SLAB, HALF), BF16),
+        pltpu.VMEM(half, BF16),
+        pltpu.VMEM((2,) + half, BF16),
+        pltpu.VMEM(half, BF16),
         pltpu.VMEM((2,) + half, BF16),
         pltpu.VMEM((2,) + half, BF16),
         pltpu.VMEM(slots, BF16),
@@ -479,8 +502,8 @@
         pltpu.VMEM((4,) + part, BF16),
         pltpu.VMEM((4,) + part, BF16),
         dma((6,)), dma, dma, dma((ladder,)),
-        dma, dma, dma, dma((ladder - 1,)), dma((ladder - 1,)), dma((ladder,)), dma((ladder - 1,)),
-        dma((2,)), dma, dma, dma((6,)), dma((6,)),
+        dma, dma, dma((ladder - 1,)), dma((ladder - 1,)), dma((ladder,)), dma((ladder - 1,)),
+        dma, dma, dma((6,)), dma((6,)),
     ]
     query_grad, key_grad, value_grad = pl.pallas_call(
         kernel,

time: 55.3 us -> 54.1 us (0.978)
  the two profiles are of different devices: /device:TPU:6 before, /device:TPU:8 now
where the time goes in v3:
time: 54.1 us; the launch traced here: 53.9 us
  Pallas kernels  53.3 us (99%)
  between operations  0.64 us (1%)
    pallas_call x1, Pallas kernels, per_device(): pl.pallas_call(kernel, out_shape=(pltpu.VMEM(slots, BF16), pltpu.VMEM(slo...  52.1 us
    pallas_call x1, Pallas kernels, per_device(): pl.pallas_call(write_out, out_shape=(jax.ShapeDtypeStruct(slots, BF16), j...  1.16 us

profile of v3, /device:TPU:8, one launch (start us, length us, event | category | flops | bytes accessed | tf_op | source)
XLA Modules:
  0.0 53.9 jit_solution(2709230759037249566)
XLA Ops:
  0.6 52.1 %fenwick_backward.1 = (bf16[8,128,128]{2,1,0:T(8,128)(2,1)S(1)}, bf16[8,128,128]{2,1,0:T(8,128)(2,1)S(1)}, bf16[1024,512]{1,0:T(8,128)(2,1)S(1)}) custom-call(bf16[1024,128]{1,0:T(8,128)(2,1)} %q_in.1, bf16[1024,128]{1,0:T(8,128)(2,1)} %k_in.1, bf16[1024,512]{1,0:T(8,128)(2,1)} %v_in.1, bf16[1024,512]{1,0:T(8,128)(2,1)} %og_in.1, s32[7,1024]{1,0:T(8,128)} %bitcast.3, ...), custom_call_target="tpu_custom_call" | custom-call | tf_op jit(solution)/shard_map/fenwick_backward/pallas_call | solution.py:508
  52.8 1.2 %write_out.1 = (bf16[8,128,128]{2,1,0:T(8,128)(2,1)}, bf16[8,128,128]{2,1,0:T(8,128)(2,1)}, bf16[1024,512]{1,0:T(8,128)(2,1)}) custom-call(bf16[8,128,128]{2,1,0:T(8,128)(2,1)S(1)} %get-tuple-element.9.q_in, bf16[8,128,128]{2,1,0:T(8,128)(2,1)S(1)} %get-tuple-element.10.k_in, bf16[1024,512]{1,0:T(8,128)(2,1)S(1)} %get-tuple-element.11.v_in), custom_call_target="tpu_custom_call" | custom-call | tf_op jit(solution)/shard_map/write_out/pallas_call | solution.py:528

commit v4 on v3

--- a/solution.py
+++ b/solution.py
@@ -36,11 +36,11 @@
     qg_ref, kg_ref, vg_ref,
     q_ref, k_ref, v_ref, og_ref, idx_ref, table_ref,
     scaled, picks, q_turned, q_acc, k_acc, v_acc,
-    b_own, b_both, a_slabs, t2_buf, t3_buf, t4_buf, far_sib, sib,
-    lg_own, lg_both, lg_sum, b_slabs, five_slabs, six_slabs, g_own, g_buf, state,
+    b_own, b_both, a_slabs, t2_buf, t3_buf, t4_buf, t4_far, t5_buf, sib,
+    lg_own, lg_both, lg_sum, b_slabs, five_slabs, six_slabs, six_own, six_far, g_own, g_buf, state,
     q_part, k_part, q_relay, k_relay, q_slots, k_slots,
     in_sem, tree_s, head_s, level_s,
-    a0_r, a1_r, a3_r, a4_r, b0_r, b1_r, b3_r, b4_r, q_r, k_r,
+    a0_r, a1_r, a2_r, b2_r, a3_r, a4_r, b0_r, b1_r, b3_r, b4_r, q_r, k_r,
 ):
     seq = lax.axis_index("seq")
     y = lax.axis_index("head")
@@ -165,13 +165,12 @@
                 zt = z_at(step)
                 part = lg_sum.at[level, zt]
                 if level == 6:
-                    targets = ((six_slabs.at[x - 2, z], at(0, zt, core)), (six_slabs.at[x - 2, z], at(1, zt, core)))
+                    slot, to = six_slabs.at[z], at(x - 2, zt, core)
                 elif level == 5:
-                    targets = ((five_slabs.at[z], at(x - 1, zt, core)),)
+                    slot, to = five_slabs.at[z], at(x - 1, zt, core)
                 else:
-                    targets = ((b_slabs.at[level, z], at(x, zt, core)),)
-                for slot, to in targets:
-                    send(part, slot, level_s.at[level - 1], b1_r.at[level - 2], to)
+                    slot, to = b_slabs.at[level, z], at(x, zt, core)
+                send(part, slot, level_s.at[level - 1], b1_r.at[level - 2], to)
             if level < 5:
                 b_slabs[level, z] = lg_sum[level, z]
 
@@ -255,16 +254,14 @@
     def keep_sibling(level):
         sib[level, core, z] = sib_src(level, z)[...]
 
-    for step in z_order + [0]:
-        zt = z_at(step)
-
-        @pl.when(lax.div(x, 2) == 0)
-        def _(zt=zt):
-            for x_to in (2, 3):
-                send(t4_buf, far_sib.at[x, z], level_s.at[5], a3_r.at[4], at(x_to, zt, core))
-
-        @pl.when(lax.rem(x, 2) == 0)
-        def _(zt=zt):
+    @pl.when(lax.div(x, 2) == 0)
+    def _():
+        send(t4_buf, t4_far, level_s.at[5], a2_r, at(1 - x, z, core))
+
+    @pl.when(lax.rem(x, 2) == 0)
+    def _():
+        for step in z_order + [0]:
+            zt = z_at(step)
             send(t4_buf, sib.at[5, core, z], level_s.at[4], a3_r.at[3], at(x + 1, zt, core))
 
     for step in z_order:
@@ -290,7 +287,27 @@
 
     block_tile(1)
 
+
+    @pl.when(lax.div(x, 2) == 0)
+    def _():
+        arrived(t4_far, a2_r)
+        t5_buf[...] = (t4_buf[...].astype(F32) + t4_far[...].astype(F32)).astype(BF16)
+        for step in z_order + [0]:
+            zt = z_at(step)
+            send(t5_buf, sib.at[6, core, z], level_s.at[5], a3_r.at[4], at(x + 2, zt, core))
+
     block_tile(2)
+
+
+    @pl.when(lax.div(x, 2) == 0)
+    def _():
+        arrived(six_slabs, b1_r.at[4])
+        total = six_slabs[0].astype(F32)
+        for i in range(1, NZ):
+            total += six_slabs[i].astype(F32)
+        six_own[...] = total.astype(BF16)
+        send(six_own, six_far, level_s.at[5], b2_r, at(1 - x, z, core))
+
     block_tile(3)
 
     for level in (2, 3, 4):
@@ -308,13 +325,12 @@
 
     @pl.when(lax.div(x, 2) == 0)
     def _():
-        arrived(six_slabs, b1_r.at[4])
+        arrived(six_far, b2_r)
 
     five = five_slabs[0].astype(F32)
-    six = six_slabs[0, 0].astype(F32) + six_slabs[1, 0].astype(F32)
+    six = six_own[...].astype(F32) + six_far[...].astype(F32)
     for i in range(1, NZ):
         five += five_slabs[i].astype(F32)
-        six += six_slabs[0, i].astype(F32) + six_slabs[1, i].astype(F32)
     zero = jnp.zeros((SLAB, HALF), F32)
     far = jnp.where(lax.rem(x, 2) == 0, five, zero) + jnp.where(lax.div(x, 2) == 0, six, zero)
     upper = b_slabs[4, 4].astype(F32)
@@ -372,14 +388,10 @@
         arrived(out.at[above], r_sem.at[4])
         send(out.at[above], out.at[above], head_s, r_sem.at[5], (seq, y_at(-1)))
 
-    for level in (6, 5, 4, 3, 2):
+    for level in (5, 4, 3, 2, 6):
         @pl.when(flag(level))
         def _(level=level):
-            if level == 6:
-                arrived(far_sib, a3_r.at[4])
-                sib[6, core] = (far_sib[0].astype(F32) + far_sib[1].astype(F32)).astype(BF16)
-            else:
-                arrived(sib.at[level, core, pl.ds(0, NZ - 1 if level < 5 else NZ)], a3_r.at[level - 2])
+            arrived(sib.at[level, core, pl.ds(0, NZ - 1 if level < 5 else NZ)], a3_r.at[level - 2])
             send(sib.at[level, core], sib.at[level, core], level_s.at[level - 1], a4_r.at[level - 2], peer)
 
     for level in (6, 5, 4, 3, 2):
@@ -429,7 +441,7 @@
     def _():
         sent(128, level_s.at[0])
 
-    for level, bytes_set, bytes_unset in ((2, 208, 32), (3, 208, 32), (4, 208, 32), (5, 192, 64), (6, 256, 128)):
+    for level, bytes_set, bytes_unset in ((2, 208, 32), (3, 208, 32), (4, 208, 32), (5, 192, 64), (6, 192, 80)):
         @pl.when(flag(level))
         def _(level=level, bytes_set=bytes_set):
             sent(bytes_set, level_s.at[level - 1])
@@ -484,14 +496,17 @@
         pltpu.VMEM((4, SLAB, HALF), BF16),
         pltpu.VMEM((SLAB, HALF), BF16),
         pltpu.VMEM((SLAB, HALF), BF16),
-        pltpu.VMEM((2,) + half, BF16),
+        pltpu.VMEM((SLAB, HALF), BF16),
+        pltpu.VMEM((SLAB, HALF), BF16),
         pltpu.VMEM((LEVELS, 2) + half, BF16),
         pltpu.VMEM((LEVELS, 2) + half, BF16),
         pltpu.VMEM((LEVELS,) + half, BF16),
         pltpu.VMEM((LEVELS,) + half, BF16),
         pltpu.VMEM((LEVELS,) + half, BF16),
         pltpu.VMEM(half, BF16),
-        pltpu.VMEM((2,) + half, BF16),
+        pltpu.VMEM(half, BF16),
+        pltpu.VMEM((SLAB, HALF), BF16),
+        pltpu.VMEM((SLAB, HALF), BF16),
         pltpu.VMEM(half, BF16),
         pltpu.VMEM((2,) + half, BF16),
         pltpu.VMEM((2,) + half, BF16),
@@ -502,7 +517,7 @@
         pltpu.VMEM((4,) + part, BF16),
         pltpu.VMEM((4,) + part, BF16),
         dma((6,)), dma, dma, dma((ladder,)),
-        dma, dma, dma((ladder - 1,)), dma((ladder - 1,)), dma((ladder,)), dma((ladder - 1,)),
+        dma, dma, dma, dma, dma((ladder - 1,)), dma((ladder - 1,)), dma((ladder,)), dma((ladder - 1,)),
         dma, dma, dma((6,)), dma((6,)),
     ]
     query_grad, key_grad, value_grad = pl.pallas_call(

time: 54.1 us -> 54.3 us (level)
  the two profiles are of different devices: /device:TPU:8 before, /device:TPU:6 now
where the time goes in v4:
time: 54.3 us; the launch traced here: 54.1 us
  Pallas kernels  53.5 us (99%)
  between operations  0.64 us (1%)
    pallas_call x1, Pallas kernels, per_device(): pl.pallas_call(kernel, out_shape=(pltpu.VMEM(slots, BF16), pltpu.VMEM(slo...  52.3 us
    pallas_call x1, Pallas kernels, per_device(): pl.pallas_call(write_out, out_shape=(jax.ShapeDtypeStruct(slots, BF16), j...  1.16 us

profile of v4, /device:TPU:6, one launch (start us, length us, event | category | flops | bytes accessed | tf_op | source)
XLA Modules:
  0.0 54.1 jit_solution(3753145728898888611)
XLA Ops:
  0.6 52.3 %fenwick_backward.1 = (bf16[8,128,128]{2,1,0:T(8,128)(2,1)S(1)}, bf16[8,128,128]{2,1,0:T(8,128)(2,1)S(1)}, bf16[1024,512]{1,0:T(8,128)(2,1)S(1)}) custom-call(bf16[1024,128]{1,0:T(8,128)(2,1)} %q_in.1, bf16[1024,128]{1,0:T(8,128)(2,1)} %k_in.1, bf16[1024,512]{1,0:T(8,128)(2,1)} %v_in.1, bf16[1024,512]{1,0:T(8,128)(2,1)} %og_in.1, s32[7,1024]{1,0:T(8,128)} %bitcast.3, ...), custom_call_target="tpu_custom_call" | custom-call | tf_op jit(solution)/shard_map/fenwick_backward/pallas_call | solution.py:523
  53.0 1.2 %write_out.1 = (bf16[8,128,128]{2,1,0:T(8,128)(2,1)}, bf16[8,128,128]{2,1,0:T(8,128)(2,1)}, bf16[1024,512]{1,0:T(8,128)(2,1)}) custom-call(bf16[8,128,128]{2,1,0:T(8,128)(2,1)S(1)} %get-tuple-element.9.q_in, bf16[8,128,128]{2,1,0:T(8,128)(2,1)S(1)} %get-tuple-element.10.k_in, bf16[1024,512]{1,0:T(8,128)(2,1)S(1)} %get-tuple-element.11.v_in), custom_call_target="tpu_custom_call" | custom-call | tf_op jit(solution)/shard_map/write_out/pallas_call | solution.py:543

commit v5 on v4

--- a/solution.py
+++ b/solution.py
@@ -15,8 +15,7 @@
 SLAB = 16
 HALF = 256
 TILE = 256
-EARLY = (6, 5, 4)
-LATE = (3, 2, 1)
+EARLY = (6, 5, 4, 3, 2)
 
 
 def rows_by_rows(left, right):
@@ -99,10 +98,10 @@
     loads[1].start()
 
     barrier = pltpu.get_barrier_semaphore()
-    for x_step in (2, 3, 1, 0):
-        for step in z_order if x_step == 0 else z_order + [0]:
+    for x_to, steps in ((x_at(2), z_order + [0]), (x + 1 - 2 * lax.rem(x, 2), z_order + [0]), (x, z_order)):
+        for step in steps:
             pl.semaphore_signal(
-                barrier, inc=1, device_id=at(x_at(x_step), z_at(step), core), device_id_type=MESH
+                barrier, inc=1, device_id=at(x_to, z_at(step), core), device_id_type=MESH
             )
     for step in (2, -2, 1, -1):
         pl.semaphore_signal(barrier, inc=1, device_id=(seq, y_at(step)), device_id_type=MESH)
@@ -177,12 +176,15 @@
     for level in EARLY:
         level_grad(level)
 
-    pl.semaphore_wait(barrier, 1 + (NX * NZ - 1) + 4)
+    pl.semaphore_wait(barrier, 1 + (3 * NZ - 1) + 4)
     send(b_own, b_both, tree_s, a0_r, peer)
     for level in EARLY:
         swap_level(level)
-    level_grad(LATE[0])
-    swap_level(LATE[0])
+    level_grad(1)
+
+    @pl.when(core == 1)
+    def _():
+        send(lg_own.at[1], state, level_s.at[0], b0_r.at[0], peer)
 
     arrived(b_both, a0_r)
     lg_sum[0] = (b_own[core].astype(F32) + b_both[core].astype(F32)).astype(BF16)
@@ -193,16 +195,6 @@
 
     for level in EARLY:
         hand_level(level)
-    for before, level in zip(LATE, LATE[1:]):
-        level_grad(level)
-        if level > 1:
-            swap_level(level)
-        hand_level(before)
-
-    @pl.when(core == 1)
-    def _():
-        send(lg_own.at[1], state, level_s.at[0], b0_r.at[0], peer)
-
     scale_level(0)
 
     def block_tile(j):

time: 54.3 us -> 54.1 us (level)
  no operation moved by 1% of the time
where the time goes in v5:
time: 54.1 us; the launch traced here: 53.9 us
  Pallas kernels  53.3 us (99%)
  between operations  0.64 us (1%)
    pallas_call x1, Pallas kernels, per_device(): pl.pallas_call(kernel, out_shape=(pltpu.VMEM(slots, BF16), pltpu.VMEM(slo...  52.1 us
    pallas_call x1, Pallas kernels, per_device(): pl.pallas_call(write_out, out_shape=(jax.ShapeDtypeStruct(slots, BF16), j...  1.16 us

profile of v5, /device:TPU:6, one launch (start us, length us, event | category | flops | bytes accessed | tf_op | source)
XLA Modules:
  0.0 53.9 jit_solution(5885739739033988165)
XLA Ops:
  0.6 52.1 %fenwick_backward.1 = (bf16[8,128,128]{2,1,0:T(8,128)(2,1)S(1)}, bf16[8,128,128]{2,1,0:T(8,128)(2,1)S(1)}, bf16[1024,512]{1,0:T(8,128)(2,1)S(1)}) custom-call(bf16[1024,128]{1,0:T(8,128)(2,1)} %q_in.1, bf16[1024,128]{1,0:T(8,128)(2,1)} %k_in.1, bf16[1024,512]{1,0:T(8,128)(2,1)} %v_in.1, bf16[1024,512]{1,0:T(8,128)(2,1)} %og_in.1, s32[7,1024]{1,0:T(8,128)} %bitcast.3, ...), custom_call_target="tpu_custom_call" | custom-call | tf_op jit(solution)/shard_map/fenwick_backward/pallas_call | solution.py:515
  52.8 1.2 %write_out.1 = (bf16[8,128,128]{2,1,0:T(8,128)(2,1)}, bf16[8,128,128]{2,1,0:T(8,128)(2,1)}, bf16[1024,512]{1,0:T(8,128)(2,1)}) custom-call(bf16[8,128,128]{2,1,0:T(8,128)(2,1)S(1)} %get-tuple-element.9.q_in, bf16[8,128,128]{2,1,0:T(8,128)(2,1)S(1)} %get-tuple-element.10.k_in, bf16[1024,512]{1,0:T(8,128)(2,1)S(1)} %get-tuple-element.11.v_in), custom_call_target="tpu_custom_call" | custom-call | tf_op jit(solution)/shard_map/write_out/pallas_call | solution.py:535
